TPU v7x, 32 devices: a whole 2x2x4 slice. The times are simulated.
32 devices in a mesh: seq: 4 (over y, x), grp: 8 (over z, core).
Axes of the slice: x: 2, y: 2, z: 4, core: 2. Of those that a mesh axis runs over, the one named last changes fastest.
Arguments:
- conv_input: bfloat16 [8, 2048, 5120], P('grp', 'seq'), may hold values from -6 to 6
- step_raw: float32 [8, 64, 2048], P('grp', None, 'seq'), may hold values from -5 to 0
- decay_rate: float32 [64], replicated, may hold values from 0 to 2, as said below
- conv_weight: bfloat16 [4, 5120], replicated, may hold values from -3 to 3
- conv_bias: bfloat16 [5120], replicated, may hold values from -3 to 3
- norm_gain: float32 [4096], replicated, may hold values from 0.5 to 1.5
- owner_slot: int32 [8], replicated, may hold values from 0 to 7, each once
Outputs:
- mixed: bfloat16 [8, 2048, 4096], P('grp', 'seq')
- final_ssm: float32 [8, 64, 64, 128], P('seq', 'grp')
- final_conv: bfloat16 [8, 5120, 4], P('seq', 'grp')
Inputs may be any that keep to these rules, and one draw needn't show every extreme that they name: `decay_rate`: positive. `owner_slot`: every decode row receives exactly one prompt.
All inputs are finite; a program needn't handle non-finite values.
Results may differ from a plain program's by a relative error of at most 0.009.
Values may be sent and summed in bfloat16 or wider, within the bound.
A program may use at most 128 MiB of HBM per device.

v0:
```python
import jax
import jax.numpy as jnp
from jax import lax
from jax.sharding import PartitionSpec as P

HEADS = 64
HEAD_DIM = 64
STATE = 128
GROUPS = 4
BLOCK = 256
D_IN = 4096


NORM_EPS = 1.0


def passed_along(block, axis, distance):
    devices = range(lax.axis_size(axis))
    route = [(i - distance, i) for i in devices if i - distance in devices]
    return lax.ppermute(block, axis, route)


def conv_silu(padded, conv_weight, conv_bias):
    width = conv_weight.shape[0]
    length = padded.shape[0] - width + 1
    total = (
        jnp.zeros((length, padded.shape[1]), jnp.float32) + conv_bias.astype(jnp.float32)[None, :]
    )
    for offset in range(width):
        total = total + conv_weight[offset].astype(jnp.float32)[None, :] * padded[
            offset : offset + length
        ].astype(jnp.float32)
    return jax.nn.silu(total).astype(jnp.bfloat16)


def block_terms(inputs, b_matrix, c_matrix, step_size, log_decay):
    width = log_decay.shape[-1]
    summed = jnp.cumsum(log_decay, axis=-1)
    scores = jnp.einsum("tgn,ugn->gtu", c_matrix, b_matrix, preferred_element_type=jnp.float32)
    causal = jnp.arange(width)[:, None] >= jnp.arange(width)[None, :]
    spread = jnp.exp(jnp.minimum(summed[:, :, :, None] - summed[:, :, None, :], 0.0))
    weights = (
        jnp.where(causal, spread, 0.0) * step_size[:, :, None, :] * scores[:, None, :, :]
    ).astype(jnp.bfloat16)
    intra = jnp.einsum("gktu,ugkp->tgkp", weights, inputs, preferred_element_type=jnp.float32)
    tail = jnp.exp(summed[:, :, -1:] - summed) * step_size
    scaled = (
        tail[..., None] * jnp.swapaxes(b_matrix, 0, 1).astype(jnp.float32)[:, None, :, :]
    ).astype(jnp.bfloat16)
    local = jnp.einsum("gkun,ugkp->gkpn", scaled, inputs, preferred_element_type=jnp.float32)
    return (intra, local, jnp.exp(summed[:, :, -1]), jnp.exp(summed))


def from_state(c_matrix, carried, scale):
    reach = jnp.einsum(
        "tgn,gkpn->tgkp", c_matrix, carried.astype(jnp.bfloat16), preferred_element_type=jnp.float32
    )
    return reach * jnp.transpose(scale, (2, 0, 1))[..., None]


def body(conv_input, step_raw, decay_rate, conv_weight, conv_bias, norm_gain, owner_slot):
    width = conv_weight.shape[0]
    own_rows = conv_input[0]
    length = own_rows.shape[0]
    before = passed_along(conv_input[:, length - width + 1 :, :], "seq", 1)
    padded = jnp.concatenate([before[0], own_rows], axis=0)
    conved = conv_silu(padded, conv_weight, conv_bias)
    blocks = length // BLOCK
    per_group = HEADS // GROUPS
    inputs = conved[:, :D_IN].reshape(blocks, BLOCK, GROUPS, per_group, HEAD_DIM)
    b_matrix = conved[:, D_IN : D_IN + GROUPS * STATE].reshape(blocks, BLOCK, GROUPS, STATE)
    c_matrix = conved[:, D_IN + GROUPS * STATE :].reshape(blocks, BLOCK, GROUPS, STATE)
    step_size = jax.nn.softplus(step_raw[0])
    log_decay = -step_size * decay_rate[:, None]
    shard_log = jnp.sum(log_decay, axis=-1).reshape(GROUPS, per_group)
    step_size = step_size.reshape(GROUPS, per_group, blocks, BLOCK)
    log_decay = log_decay.reshape(GROUPS, per_group, blocks, BLOCK)
    pieces = []
    end_state = jnp.zeros((GROUPS, per_group, HEAD_DIM, STATE), jnp.float32)
    for number in range(blocks):
        terms = block_terms(
            inputs[number],
            b_matrix[number],
            c_matrix[number],
            step_size[:, :, number],
            log_decay[:, :, number],
        )
        pieces.append(terms)
        end_state = terms[2][:, :, None, None] * end_state + terms[1]
    shard_decay = jnp.exp(shard_log)

    def relay_step(turn, carry):
        incoming = passed_along(carry[0], "seq", 1)
        return (shard_decay[:, :, None, None] * incoming + end_state, incoming)

    outgoing, incoming = lax.fori_loop(
        0, lax.axis_size("seq") - 1, relay_step, (end_state, jnp.zeros_like(end_state))
    )
    carried = incoming
    outputs = []
    for number in range(blocks):
        intra, local, decay, scale = pieces[number]
        outputs.append(intra + from_state(c_matrix[number], carried, scale))
        carried = decay[:, :, None, None] * carried + local
    values = jnp.concatenate(outputs, axis=0).reshape(length, GROUPS, per_group * HEAD_DIM)
    norm_scale = lax.rsqrt(jnp.mean(values * values, axis=-1) + NORM_EPS)
    mixed = ((values * norm_scale[..., None]).reshape(length, D_IN) * norm_gain[None, :]).astype(
        jnp.bfloat16
    )[None]
    place = lax.axis_index("seq")
    last = lax.axis_size("seq") - 1
    kept = jnp.transpose(own_rows[length - width :], (1, 0)).astype(jnp.float32)[None]
    shard_logs = lax.all_gather(shard_log[None], "seq", axis=0, tiled=True)
    after = jnp.arange(shard_logs.shape[0]) > place
    later_log = jnp.sum(jnp.where(after[:, None, None], shard_logs, 0.0), axis=0)
    sent_state = (jnp.exp(later_log)[:, :, None, None] * end_state).reshape(
        1, HEADS, HEAD_DIM, STATE
    )
    sent_conv = jnp.where(place == last, kept, 0.0)
    got_state, got_conv = (
        lax.all_to_all(sent_state, "grp", split_axis=1, concat_axis=0, tiled=True),
        lax.all_to_all(sent_conv, "grp", split_axis=1, concat_axis=0, tiled=True),
    )
    placed_state = jnp.zeros_like(got_state).at[owner_slot].set(got_state)
    placed_conv = jnp.zeros_like(got_conv).at[owner_slot].set(got_conv)
    final_ssm, summed_conv = (
        lax.psum_scatter(
            placed_state.astype(jnp.bfloat16), "seq", scatter_dimension=0, tiled=True
        ).astype(jnp.float32),
        lax.psum_scatter(
            placed_conv.astype(jnp.bfloat16), "seq", scatter_dimension=0, tiled=True
        ).astype(jnp.float32),
    )
    final_conv = summed_conv.astype(jnp.bfloat16)
    return (mixed, final_ssm, final_conv)


def solution(mesh):
    placed = (P("grp", "seq", None), P("grp", None, "seq"), P(), P(), P(), P(), P())
    return jax.shard_map(
        body,
        mesh=mesh,
        in_specs=placed,
        out_specs=(P("grp", "seq", None), P("seq", "grp", None, None), P("seq", "grp", None)),
        check_vma=False,
    )
```

profile of v0, /device:TPU:0, one launch (start us, length us, event | category | flops | bytes accessed | tf_op | source)
XLA Modules:
  0.0 379.2 jit_solution(1208583587146269343)
XLA Ops:
  7.2 0.9 slice.96
  8.1 4.9 %collective-permute-start.1 = (bf16[1,3,5120]{2,1,0:T(4,128)(2,1)S(1)}, bf16[1,3,5120]{2,1,0:T(4,128)(2,1)S(1)}, u32[]{:S(2)}, u32[]{:S(2)}) collective-permute-start(bf16[1,3,5120]{2,1,0:T(4,128)(2,1)S(1)} %slice.96), channel_id=1, source_target_pairs={{0,8},{8,16},{16,24},{1,9},{9,17},{17,25},{2,10},{10,18},{18,26},{... | collective-permute-start | bytes 92168 | tf_op jit(solution)/shard_map/ppermute | solution.py:20
  13.0 0.9 slice_convert_fusion
  13.9 0.7 mul.256
  14.7 1.1 fusion.30
  15.8 1.0 squeeze.50
  16.8 1.2 compare_select_fusion.2
  18.1 8.1 %all_gather.3 = f32[4,4,16]{2,1,0:T(4,128)S(1)} all-gather(f32[1,4,16]{2,1,0:T(4,128)S(1)} %broadcast_in_dim_reshape.3), channel_id=1, replica_groups=mesh['seq'=4,'grp'=8] {'seq'}, dimensions={0}, use_global_device_ids=true | all-gather | bytes 1280 | tf_op jit(solution)/shard_map/all_gather | solution.py:113
  26.2 1.0 slice_convert_fusion.4
  27.8 2.3 reduce-window.14
  30.1 2.3 reduce-window.16
  33.3 0.8 exponential_bitcast_fusion.1
  34.1 0.8 copy.110
  34.9 0.7 exponential_bitcast_fusion
  35.6 1.7 broadcast_select_fusion
  37.4 8.0 %copy.90 = bf16[1,512,5120]{1,2,0:T(8,128)(2,1)} copy(bf16[1,512,5120]{2,1,0:T(8,128)(2,1)} %param.9) | data formatting | bytes 10485760 | tf_op args[0]
  45.4 0.6 exp.78
  46.0 0.6 broadcast.133
  46.6 23.4 %reduce.5 = f32[5120,4]{1,0:T(8,128)S(1)} reduce(f32[5120,1,4]{2,1,0:T(1,128)} %bitcast.123, f32[]{:T(128)} %broadcast.133), dimensions={1}, to_apply=%bitcast.100.reduce_sub_computation | reduce | bytes 163844
  70.1 2.9 reshape.258
  73.0 0.6 dynamic-slice
  74.2 0.6 copy.89
  74.8 18.1 %multiply_convert_fusion.2 = bf16[512,5120]{0,1:T(8,128)(2,1)S(1)} fusion(bf16[512,5120]{0,1:T(8,128)(2,1)} %bitcast.121, bf16[3,5120]{0,1:T(8,128)(2,1)S(1)} %bitcast.126, f32[5120]{0:T(1024)S(1)} %bitcast.141, f32[5120]{0:T(1024)S(1)} %bitcast.142, f32[5120]{0:T(1024)S(1)} %bitcast.140, f32[5120]{0:T(1024)S(1)} %bitcast.139, f32[5120]{0:T(1024)S(1)} %convert_element_type.82), kind=kLoop, calls=%fused_computation.5 | loop fusion | flops 68157440 | bytes 10618880 | tf_op jit(solution)/shard_map/convert_element_type | solution.py:33
  93.0 1.6 fusion.42
  94.7 0.9 convert_bitcast_fusion.1
  95.5 2.0 copy.101
  97.6 0.8 convert_bitcast_fusion
  98.4 2.1 copy.102
  100.5 1.3 fusion.47
  101.8 1.3 fusion.46
  103.1 4.8 %fusion.16 = f32[4,16,64,128]{3,2,1,0:T(8,128)S(1)} fusion(bf16[256,4,16,64]{0,3,2,1:T(8,128)(2,1)} %bitcast.135, f32[4,256,128]{2,1,0:T(8,128)} %copy.101, f32[4,16,256]{2,1,0:T(8,128)} %get-tuple-element.55), kind=kOutput, calls=%fused_computation.32 | convolution fusion | flops 272629760 | bytes 4784128 | tf_op jit(solution)/shard_map/gkun,ugkp->gkpn/dot_general | solution.py:50
  108.0 4.8 %broadcast_multiply_fusion = (f32[4,16,64,128]{3,2,1,0:T(8,128)}, f32[4,16,64,128]{3,2,1,0:T(8,128)}) fusion(f32[4,16]{1,0:T(4,128)S(1)} %copy-done.14, bf16[256,4,16,64]{0,3,2,1:T(8,128)(2,1)S(1)} %bitcast.124, f32[4,256,128]{2,1,0:T(8,128)S(1)} %copy-done.6, f32[4,16,256]{2,1,0:T(8,128)S(1)} %get-tuple-element.57, f32[4,16,64,128]{3,2,1,0:T(8,128)S(1)} %fusion.16, ...), kind=kOutput, calls=%fused_computation.46 | convolution fusion | flops 274726912 | bytes 8979200 | tf_op jit(solution)/shard_map/gkun,ugkp->gkpn/dot_general | solution.py:50
  112.7 4.9 %all-to-all-start = ((f32[1,64,64,128]{3,2,0,1:T(8,128)}), f32[1,64,64,128]{3,2,0,1:T(8,128)}, u32[]{:S(2)}, u32[]{:S(2)}) async-start(f32[1,64,64,128]{3,2,0,1:T(8,128)} %bitcast.29), calls=%async_computation | async-start | bytes 4194304 | tf_op jit(solution)/shard_map/all_to_all | solution.py:121
  117.6 3.2 copy.145
  120.8 157.9 %while.12 = (s32[]{:T(128)}, f32[4,16,64,128]{3,2,1,0:T(8,128)}, f32[4,16,64,128]{3,2,1,0:T(8,128)}, f32[4,16]{1,0:T(4,128)S(1)}, f32[4,16,64,128]{3,2,1,0:T(8,128)}, /*index=5*/s32[]{:T(128)}) while((s32[]{:T(128)}, f32[4,16,64,128]{3,2,1,0:T(8,128)}, f32[4,16,64,128]{3,2,1,0:T(8,128)}, f32[4,16]{1,0:T(4,128)S(1)}, ...), condition=%wide.region_6.7_spmd, body=%wide.region_5.6_spmd.sunk | while | flops 1048578 | bytes 23069064 | solution.py:96
  120.8 2.5 collective-permute-start
  123.4 45.7 %collective-permute-done = f32[4,16,64,128]{3,2,1,0:T(8,128)S(1)} collective-permute-done((f32[4,16,64,128]{3,2,1,0:T(8,128)}, f32[4,16,64,128]{3,2,1,0:T(8,128)S(1)}, u32[]{:S(2)}, u32[]{:S(2)}) %collective-permute-start) | collective-permute-done | bytes 2097184 | tf_op jit(solution)/shard_map/while/body/eval_jaxpr/ppermute | solution.py:20
  169.1 4.0 %multiply_add_fusion.3 = f32[4,16,64,128]{3,2,1,0:T(8,128)} fusion(f32[4,16,64,128]{3,2,1,0:T(8,128)} %get-tuple-element.113, f32[4,16,64,128]{3,2,1,0:T(8,128)S(1)} %collective-permute-done, f32[4,16]{1,0:T(4,128)S(1)} %get-tuple-element.112), kind=kLoop, calls=%fused_computation.2.clone.1 | loop fusion | flops 1048576 | bytes 6291712 | tf_op jit(solution)/shard_map/while/body/eval_jaxpr/add | solution.py:94
  173.1 4.4 %collective-permute-start = (f32[4,16,64,128]{3,2,1,0:T(8,128)}, f32[4,16,64,128]{3,2,1,0:T(8,128)S(1)}, u32[]{:S(2)}, u32[]{:S(2)}) collective-permute-start(f32[4,16,64,128]{3,2,1,0:T(8,128)} %get-tuple-element.104), channel_id=1, source_target_pairs={{0,8},{8,16},{16,24},{1,9},{9,17},{17,25},{2,10},{10,18},{18,26},{... | collective-permute-start | bytes 6291464 | tf_op jit(solution)/shard_map/while/body/eval_jaxpr/ppermute | solution.py:20
  177.5 44.9 %collective-permute-done = f32[4,16,64,128]{3,2,1,0:T(8,128)S(1)} collective-permute-done((f32[4,16,64,128]{3,2,1,0:T(8,128)}, f32[4,16,64,128]{3,2,1,0:T(8,128)S(1)}, u32[]{:S(2)}, u32[]{:S(2)}) %collective-permute-start) | collective-permute-done | bytes 2097184 | tf_op jit(solution)/shard_map/while/body/eval_jaxpr/ppermute | solution.py:20
  222.3 4.0 %multiply_add_fusion.3 = f32[4,16,64,128]{3,2,1,0:T(8,128)} fusion(f32[4,16,64,128]{3,2,1,0:T(8,128)} %get-tuple-element.113, f32[4,16,64,128]{3,2,1,0:T(8,128)S(1)} %collective-permute-done, f32[4,16]{1,0:T(4,128)S(1)} %get-tuple-element.112), kind=kLoop, calls=%fused_computation.2.clone.1 | loop fusion | flops 1048576 | bytes 6291712 | tf_op jit(solution)/shard_map/while/body/eval_jaxpr/add | solution.py:94
  226.3 4.4 %collective-permute-start = (f32[4,16,64,128]{3,2,1,0:T(8,128)}, f32[4,16,64,128]{3,2,1,0:T(8,128)S(1)}, u32[]{:S(2)}, u32[]{:S(2)}) collective-permute-start(f32[4,16,64,128]{3,2,1,0:T(8,128)} %get-tuple-element.104), channel_id=1, source_target_pairs={{0,8},{8,16},{16,24},{1,9},{9,17},{17,25},{2,10},{10,18},{18,26},{... | collective-permute-start | bytes 6291464 | tf_op jit(solution)/shard_map/while/body/eval_jaxpr/ppermute | solution.py:20
  230.7 44.0 %collective-permute-done = f32[4,16,64,128]{3,2,1,0:T(8,128)S(1)} collective-permute-done((f32[4,16,64,128]{3,2,1,0:T(8,128)}, f32[4,16,64,128]{3,2,1,0:T(8,128)S(1)}, u32[]{:S(2)}, u32[]{:S(2)}) %collective-permute-start) | collective-permute-done | bytes 2097184 | tf_op jit(solution)/shard_map/while/body/eval_jaxpr/ppermute | solution.py:20
  274.7 4.0 %multiply_add_fusion.3 = f32[4,16,64,128]{3,2,1,0:T(8,128)} fusion(f32[4,16,64,128]{3,2,1,0:T(8,128)} %get-tuple-element.113, f32[4,16,64,128]{3,2,1,0:T(8,128)S(1)} %collective-permute-done, f32[4,16]{1,0:T(4,128)S(1)} %get-tuple-element.112), kind=kLoop, calls=%fused_computation.2.clone.1 | loop fusion | flops 1048576 | bytes 6291712 | tf_op jit(solution)/shard_map/while/body/eval_jaxpr/add | solution.py:94
  278.7 2.4 fusion.26
  281.6 0.8 fusion.24
  282.3 0.8 copy-done.5
  283.4 6.8 %fusion.18 = f32[256,4,16,64]{0,3,2,1:T(8,128)} fusion(f32[4,16,64,256]{3,2,1,0:T(8,128)S(1)} %fusion.24, bf16[256,4,16,64]{0,3,2,1:T(8,128)(2,1)S(1)} %bitcast.125, f32[4,256,256]{2,1,0:T(8,128)S(1)} %copy-done.9, f32[4,16,256]{2,1,0:T(8,128)S(1)} %bitcast.144, f32[4,16,256]{2,1,0:T(8,128)S(1)} %copy_bitcast_fusion, ...), kind=kOutput, calls=%fused_computation.35 | convolution fusion | flops 564133888 | bytes 11796480 | tf_op jit(solution)/shard_map/gktu,ugkp->tgkp/dot_general | solution.py:45
  290.2 6.8 %fusion.19 = f32[256,4,16,64]{0,3,2,1:T(8,128)} fusion(f32[4,16,64,256]{3,2,1,0:T(8,128)S(1)} %fusion.26, bf16[256,4,16,64]{0,3,2,1:T(8,128)(2,1)S(1)} %bitcast.136, f32[4,256,256]{2,1,0:T(8,128)S(1)} %copy-done.8, f32[4,16,256]{2,1,0:T(8,128)S(1)} %bitcast.143, f32[4,16,256]{2,1,0:T(8,128)S(1)} %copy_bitcast_fusion.1, ...), kind=kOutput, calls=%fused_computation.37 | convolution fusion | flops 564133888 | bytes 11796480 | tf_op jit(solution)/shard_map/gktu,ugkp->tgkp/dot_general | solution.py:45
  297.0 3.9 %all-to-all-start.1 = ((f32[8,1,2560]{2,1,0:T(1,128)}), f32[8,1,2560]{2,1,0:T(1,128)S(1)}, u32[]{:S(2)}, u32[]{:S(2)}) async-start(f32[8,1,2560]{2,1,0:T(1,128)} %reshape.258), calls=%async_computation.2 | async-start | bytes 163840 | tf_op jit(solution)/shard_map/all_to_all | solution.py:122
  301.2 2.5 scatter_fusion
  303.7 1.3 convert_element_type.99
  305.0 6.2 %multiply_reduce_fusion = (f32[512,4]{0,1:T(4,128)S(1)}, f32[512,4,16,64]{0,3,2,1:T(8,128)}) fusion(f32[256,4,16,64]{0,3,2,1:T(8,128)} %fusion.18, f32[256,4,16,64]{0,3,2,1:T(8,128)} %fusion.19), kind=kLoop, calls=%fused_computation.12 | loop fusion | flops 6289408 | bytes 16785408 | tf_op jit(solution)/shard_map/reduce_sum | solution.py:106
  311.2 9.0 %copy.108 = f32[1,512,4096]{2,1,0:T(8,128)} copy(f32[1,512,4096]{1,2,0:T(8,128)} %bitcast.120) | data formatting | bytes 16777216 | tf_op jit(solution)/shard_map/reshape | solution.py:105
  320.4 4.4 %mul.289 = f32[512,4,1024]{2,1,0:T(4,128)} broadcast(f32[512,4]{1,0:T(8,128)S(1)} %copy.107), dimensions={0,1} | broadcast | bytes 8396800 | tf_op jit(solution)/shard_map/mul | solution.py:107
  324.7 11.0 %mul.290 = f32[1,512,4096]{2,1,0:T(8,128)} reshape(f32[512,4,1024]{2,1,0:T(4,128)} %mul.289) | data formatting | bytes 16777216 | tf_op jit(solution)/shard_map/mul | solution.py:107
  335.7 9.9 %multiply_convert_fusion.5 = bf16[1,512,4096]{2,1,0:T(8,128)(2,1)} fusion(f32[1,512,4096]{2,1,0:T(8,128)} %copy.108, f32[1,512,4096]{2,1,0:T(8,128)} %mul.290, f32[4096]{0:T(1024)S(1)} %copy-done.12), kind=kLoop, calls=%fused_computation.11 | loop fusion | flops 6291456 | bytes 20987904 | tf_op jit(solution)/shard_map/convert_element_type | solution.py:107
  345.6 0.9 reduce.6
  346.5 3.8 %reshape.259 = f32[5120,1,4]{2,1,0:T(1,128)S(1)} reshape(f32[8,2560]{1,0:T(8,128)S(1)} %reduce.6) | data formatting | bytes 163840
  350.3 0.8 copy.111
  351.1 0.7 scatter_fusion.1
  351.9 18.1 %all-reduce = bf16[8,640,4]{1,2,0:T(4,128)(2,1)S(1)} all-reduce(bf16[8,640,4]{1,2,0:T(4,128)(2,1)S(1)} %convert_element_type.102), channel_id=3, replica_groups=mesh['seq'=4,'grp'=8] {'seq'}, use_global_device_ids=true, to_apply=%region_12.13.clone | all-reduce | flops 20480 | bytes 81920
  370.0 0.6 constant_dynamic-slice_fusion
  370.6 1.8 convert_element_type.100
  (79 shorter events, 3.1 us)
Async XLA Ops:
  8.1 66.1 %collective-permute-start.1 = (bf16[1,3,5120]{2,1,0:T(4,128)(2,1)S(1)}, bf16[1,3,5120]{2,1,0:T(4,128)(2,1)S(1)}, u32[]{:S(2)}, u32[]{:S(2)}) collective-permute-start(bf16[1,3,5120]{2,1,0:T(4,128)(2,1)S(1)} %slice.96), channel_id=1, source_target_pairs={{0,8},{8,16},{16,24},{1,9},{9,17},{17,25},{2,10},{10,18},{18,26},{... | collective-permute-start | bytes 92168 | tf_op jit(solution)/shard_map/ppermute | solution.py:20
  37.4 8.6 %copy-start.13 = (bf16[5120]{0:T(1024)(128)(2,1)S(1)}, bf16[5120]{0:T(1024)(128)(2,1)}, u32[]{:S(2)}) copy-start(bf16[5120]{0:T(1024)(128)(2,1)} %param.13) | copy-start | bytes 30724
  45.4 27.6 %copy-start.16 = (u32[32]{0:T(128)S(1)}, u32[32]{0:T(128)}, u32[]{:S(2)}) copy-start(u32[32]{0:T(128)} %constant.39) | copy-start | bytes 388
  94.6 13.3 %copy-start.4 = (bf16[256,4096]{0,1:T(8,128)(2,1)}, bf16[256,4096]{0,1:T(8,128)(2,1)S(1)}, u32[]{:S(2)}) copy-start(bf16[256,4096]{0,1:T(8,128)(2,1)S(1)} %get-tuple-element.48) | copy-start | bytes 6291460
  103.1 4.8 %copy-start.6 = (f32[4,256,128]{2,1,0:T(8,128)S(1)}, f32[4,256,128]{2,1,0:T(8,128)}, u32[]{:S(2)}) copy-start(f32[4,256,128]{2,1,0:T(8,128)} %copy.102) | copy-start | bytes 1572868
  103.1 4.8 %copy-start.14 = (f32[4,16]{1,0:T(4,128)S(1)}, f32[4,16]{1,0:T(4,128)}, u32[]{:S(2)}) copy-start(f32[4,16]{1,0:T(4,128)} %exp.78) | copy-start | bytes 772
  107.9 4.8 %copy-start.2 = (f32[4,16,64,128]{3,2,1,0:T(8,128)}, f32[4,16,64,128]{3,2,1,0:T(8,128)S(1)}, u32[]{:S(2)}) copy-start(f32[4,16,64,128]{3,2,1,0:T(8,128)S(1)} %fusion.16) | copy-start | bytes 6291460
  112.7 184.3 %all-to-all-start = ((f32[1,64,64,128]{3,2,0,1:T(8,128)}), f32[1,64,64,128]{3,2,0,1:T(8,128)}, u32[]{:S(2)}, u32[]{:S(2)}) async-start(f32[1,64,64,128]{3,2,0,1:T(8,128)} %bitcast.29), calls=%async_computation | async-start | bytes 4194304 | tf_op jit(solution)/shard_map/all_to_all | solution.py:121
  120.8 48.3 %collective-permute-start = (f32[4,16,64,128]{3,2,1,0:T(8,128)}, f32[4,16,64,128]{3,2,1,0:T(8,128)S(1)}, u32[]{:S(2)}, u32[]{:S(2)}) collective-permute-start(f32[4,16,64,128]{3,2,1,0:T(8,128)} %get-tuple-element.104), channel_id=1, source_target_pairs={{0,8},{8,16},{16,24},{1,9},{9,17},{17,25},{2,10},{10,18},{18,26},{... | collective-permute-start | bytes 6291464 | tf_op jit(solution)/shard_map/while/body/eval_jaxpr/ppermute | solution.py:20
  169.1 4.0 %copy-start = (f32[4,16,64,128]{3,2,1,0:T(8,128)}, f32[4,16,64,128]{3,2,1,0:T(8,128)S(1)}, u32[]{:S(2)}) copy-start(f32[4,16,64,128]{3,2,1,0:T(8,128)S(1)} %collective-permute-done) | copy-start | bytes 6291460 | tf_op jit(solution)/shard_map/while
  173.1 49.3 %collective-permute-start = (f32[4,16,64,128]{3,2,1,0:T(8,128)}, f32[4,16,64,128]{3,2,1,0:T(8,128)S(1)}, u32[]{:S(2)}, u32[]{:S(2)}) collective-permute-start(f32[4,16,64,128]{3,2,1,0:T(8,128)} %get-tuple-element.104), channel_id=1, source_target_pairs={{0,8},{8,16},{16,24},{1,9},{9,17},{17,25},{2,10},{10,18},{18,26},{... | collective-permute-start | bytes 6291464 | tf_op jit(solution)/shard_map/while/body/eval_jaxpr/ppermute | solution.py:20
  222.3 4.0 %copy-start = (f32[4,16,64,128]{3,2,1,0:T(8,128)}, f32[4,16,64,128]{3,2,1,0:T(8,128)S(1)}, u32[]{:S(2)}) copy-start(f32[4,16,64,128]{3,2,1,0:T(8,128)S(1)} %collective-permute-done) | copy-start | bytes 6291460 | tf_op jit(solution)/shard_map/while
  226.3 48.4 %collective-permute-start = (f32[4,16,64,128]{3,2,1,0:T(8,128)}, f32[4,16,64,128]{3,2,1,0:T(8,128)S(1)}, u32[]{:S(2)}, u32[]{:S(2)}) collective-permute-start(f32[4,16,64,128]{3,2,1,0:T(8,128)} %get-tuple-element.104), channel_id=1, source_target_pairs={{0,8},{8,16},{16,24},{1,9},{9,17},{17,25},{2,10},{10,18},{18,26},{... | collective-permute-start | bytes 6291464 | tf_op jit(solution)/shard_map/while/body/eval_jaxpr/ppermute | solution.py:20
  274.7 4.0 %copy-start = (f32[4,16,64,128]{3,2,1,0:T(8,128)}, f32[4,16,64,128]{3,2,1,0:T(8,128)S(1)}, u32[]{:S(2)}) copy-start(f32[4,16,64,128]{3,2,1,0:T(8,128)S(1)} %collective-permute-done) | copy-start | bytes 6291460 | tf_op jit(solution)/shard_map/while
  278.7 2.4 copy-start.1
  278.7 2.9 copy-start.3
  281.6 1.6 copy-start.5
  281.6 1.9 copy-start.9
  281.6 1.9 copy-start.11
  283.4 6.8 %copy-start.7 = (bf16[256,4096]{0,1:T(8,128)(2,1)S(1)}, bf16[256,4096]{0,1:T(8,128)(2,1)}, u32[]{:S(2)}) copy-start(bf16[256,4096]{0,1:T(8,128)(2,1)} %get-tuple-element.49) | copy-start | bytes 6291460
  283.4 6.8 %copy-start.8 = (f32[4,256,256]{2,1,0:T(8,128)S(1)}, f32[4,256,256]{2,1,0:T(8,128)}, u32[]{:S(2)}) copy-start(f32[4,256,256]{2,1,0:T(8,128)} %fusion.46) | copy-start | bytes 3145732
  283.4 6.8 %copy-start.10 = (f32[256,4,16]{0,2,1:T(8,128)S(1)}, f32[256,4,16]{0,2,1:T(8,128)}, u32[]{:S(2)}) copy-start(f32[256,4,16]{0,2,1:T(8,128)} %get-tuple-element.54) | copy-start | bytes 196612
  290.2 11.0 %copy-start.15 = (s32[8]{0:T(128)S(1)}, s32[8]{0:T(128)}, u32[]{:S(2)}) copy-start(s32[8]{0:T(128)} %compare_select_fusion.2) | copy-start | bytes 100
  297.0 48.6 %all-to-all-start.1 = ((f32[8,1,2560]{2,1,0:T(1,128)}), f32[8,1,2560]{2,1,0:T(1,128)S(1)}, u32[]{:S(2)}, u32[]{:S(2)}) async-start(f32[8,1,2560]{2,1,0:T(1,128)} %reshape.258), calls=%async_computation.2 | async-start | bytes 163840 | tf_op jit(solution)/shard_map/all_to_all | solution.py:122
  300.9 69.7 %reduce-scatter.2.cloned.1.call-start = ((), (), s32[]{:S(2)}) async-start(), calls=%async_computation.3 | async-start | bytes 1310720 | tf_op jit(solution)/shard_map/reduce_scatter | solution.py:127
  324.7 11.0 %copy-start.12 = (f32[4096]{0:T(1024)S(1)}, f32[4096]{0:T(1024)}, u32[]{:S(2)}) copy-start(f32[4096]{0:T(1024)} %param.14) | copy-start | bytes 49156
Sparse Core Ops, SparseCore 0:
  305.2 32.0 reduce-scatter.1
where the time goes:
time: 381 us; the launch traced here: 379 us
  waiting for transfers between devices  135 us (35%)
  other arithmetic  87.8 us (23%)
  local copies, waits for them, and re-layouts  61.6 us (16%)
  matrix products  28.9 us (8%)
  blocking collectives  26.1 us (7%)
  starting transfers between devices  25.1 us (7%)
  between operations  15.1 us (4%)
    ppermute x4, waiting for transfers between devices, passed_along(): return lax.ppermute(block, axis, route)  135 us
    unnamed x1, other arithmetic  23.4 us
    unnamed x41, local copies, waits for them, and re-layouts  21.2 us
    convert_element_type x1, other arithmetic, conv_silu(): return jax.nn.silu(total).astype(jnp.bfloat16)  18.1 us
    unnamed x1, blocking collectives  18.1 us
    ppermute x4, starting transfers between devices, passed_along(): return lax.ppermute(block, axis, route)  16.2 us
    mul x2, local copies, waits for them, and re-layouts, body(): values * norm_scale[..., None]  15.4 us
    dot_general x2, matrix products, block_terms(): jnp.einsum('gktu,ugkp->tgkp', weights, inputs, preferred_element_type=jnp...  13.5 us
  transfers between devices with their start and end apart: 7, of which 3 were waited for; matrix products, arithmetic and copies ran while one was open for 36% of the time, Pallas kernels for 0%

commit v1 on v0

v1 whole, which is shorter than its diff:
```python
import functools
import math

import jax
import jax.numpy as jnp
from jax import lax
from jax.experimental import pallas as pl
from jax.experimental.pallas import tpu as pltpu
from jax.sharding import PartitionSpec as P

HEAD_DIM = 64
STATE = 128
GROUPS = 4
SUB = 128
HALO = 8
NORM_EPS = 1.0
LOG2E = math.log2(math.e)
F32 = jnp.float32
BF16 = jnp.bfloat16
NEG = -1e30


def split_rows(value):
    high = value.astype(BF16).astype(F32)
    return jnp.concatenate([high, value - high], axis=0).T.astype(BF16)


def step_kernel(raw_ref, rate_ref, col_ref, row_ref, tail_ref, near_ref, full_ref, log_ref):
    heads, length = raw_ref.shape
    per = heads // GROUPS
    u = lax.broadcasted_iota(jnp.int32, (SUB, SUB), 0)
    t = lax.broadcasted_iota(jnp.int32, (SUB, SUB), 1)
    upper = jnp.where(u <= t, 1.0, 0.0).astype(F32)
    base = jnp.zeros((heads, 1), F32)
    for j in range(length // SUB):
        cut = slice(j * SUB, (j + 1) * SUB)
        raw = raw_ref[:, cut]
        dt = jnp.maximum(raw, 0.0) + jnp.log(1.0 + jnp.exp(-jnp.abs(raw)))
        rate = dt * (rate_ref[...] * -LOG2E)
        cs = jnp.dot(rate, upper, precision=lax.Precision.HIGHEST, preferred_element_type=F32)
        q = cs - jnp.log(dt) * LOG2E
        row_ref[:, cut] = q
        total = cs[:, SUB - 1 :]
        turned = cs.T
        for g in range(GROUPS):
            col_ref[g, cut, :] = turned[:, g * per : (g + 1) * per]
        tail_ref[cut, :] = split_rows(jnp.exp2(total - q))
        near_ref[cut, :] = split_rows(jnp.exp2(cs))
        full_ref[cut, :] = split_rows(jnp.exp2(cs + base))
        base = base + total
    log_ref[...] = base


def conv_silu(buf, w_ref, b_ref, cols):
    total = b_ref[:, cols].astype(F32)
    width = w_ref.shape[0]
    for k in range(width):
        start = HALO - width + 1 + k
        total = total + w_ref[k : k + 1, cols].astype(F32) * buf[start : start + SUB, cols]
    half = 0.5 * total
    return half + half * jnp.tanh(half)


def state_kernel(
    x_ref, b_ref, c_ref, hx_ref, hb_ref, hc_ref, wx_ref, wb_ref, wc_ref, bx_ref, bb_ref, bc_ref,
    tail_ref, near_ref, exp_ref, xo_ref, bo_ref, co_ref, prev_ref, end_ref, endt_ref,
    state, xbuf, bbuf, cbuf,
):
    j = pl.program_id(1)
    last = pl.num_programs(1) - 1
    trios = ((xbuf, x_ref, hx_ref), (bbuf, b_ref, hb_ref), (cbuf, c_ref, hc_ref))

    @pl.when(j == 0)
    def _():
        state[...] = jnp.zeros_like(state)
        for buf, _, h_ref in trios:
            buf[:HALO, :] = h_ref[...].astype(F32)

    @pl.when(j > 0)
    def _():
        for buf, _, _ in trios:
            buf[:HALO, :] = buf[SUB:, :]

    for buf, ref, _ in trios:
        buf[HALO:, :] = ref[...].astype(F32)
    whole = slice(0, STATE)
    b = conv_silu(bbuf, wb_ref, bb_ref, whole).astype(BF16)
    bo_ref[...] = b
    co_ref[...] = conv_silu(cbuf, wc_ref, bc_ref, whole).astype(BF16)
    wide = x_ref.shape[1]
    for n in range(wide // 256):
        cols = slice(n * 256, (n + 1) * 256)
        tail = jnp.dot(tail_ref[...], exp_ref[:, cols], preferred_element_type=F32)
        decay = jnp.dot(near_ref[SUB - 8 :, :], exp_ref[:, cols], preferred_element_type=F32)[7:8, :]
        x = conv_silu(xbuf, wx_ref, bx_ref, cols).astype(BF16)
        xo_ref[:, cols] = x
        scaled = (x.astype(F32) * tail).astype(BF16)
        local = lax.dot_general(b, scaled, (((0,), (0,)), ((), ())), preferred_element_type=F32)
        old = state[:, cols]
        prev_ref[0, :, cols] = old.astype(BF16)
        state[:, cols] = decay * old + local

    @pl.when(j == last)
    def _():
        end_ref[...] = state[...].astype(BF16)
        for n in range(wide // 128):
            cols = slice(n * 128, (n + 1) * 128)
            endt_ref[cols, :] = state[:, cols].T


def intra_kernel(x_ref, b_ref, c_ref, prev_ref, col_ref, row_ref, near_ref, exp_ref, y_ref):
    b, c = b_ref[...], c_ref[...]
    scores = lax.dot_general(c, b, (((1,), (1,)), ((), ())), preferred_element_type=F32)
    t = lax.broadcasted_iota(jnp.int32, (SUB, SUB), 0)
    u = lax.broadcasted_iota(jnp.int32, (SUB, SUB), 1)
    causal = u <= t
    low = lax.broadcasted_iota(jnp.int32, (SUB, 2 * HEAD_DIM), 1) < HEAD_DIM
    zero = jnp.zeros((SUB, 2 * HEAD_DIM), BF16)
    wide = x_ref.shape[1]
    for n in range(wide // (2 * HEAD_DIM)):
        cols = slice(n * 128, (n + 1) * 128)
        parts = []
        for k in (2 * n, 2 * n + 1):
            gap = col_ref[0, :, k : k + 1] - row_ref[k : k + 1, :]
            parts.append((jnp.exp2(jnp.where(causal, gap, NEG)) * scores).astype(BF16))
        x = x_ref[:, cols]
        pair = jnp.concatenate([jnp.where(low, x, zero), jnp.where(low, zero, x)], axis=0)
        weights = jnp.concatenate(parts, axis=1)
        y = jnp.dot(weights, pair, preferred_element_type=F32)
        reach = jnp.dot(c, prev_ref[0, :, cols], preferred_element_type=F32)
        near = jnp.dot(near_ref[...], exp_ref[:, cols], preferred_element_type=F32)
        y_ref[:, cols] = y + near * reach


def norm_kernel(hops, y_ref, c_ref, full_ref, exp_ref, coef_ref, gain_ref, *rest):
    got, out_ref, state, buf = rest[:hops], rest[hops], rest[hops + 1], rest[hops + 2]

    @pl.when(pl.program_id(1) == 0)
    def _():
        total = coef_ref[0:1, :] * got[0][...].astype(F32)
        for k in range(1, hops):
            total = total + coef_ref[k : k + 1, :] * got[k][...].astype(F32)
        state[...] = total.astype(BF16)

    wide = y_ref.shape[1]
    squares = jnp.zeros((SUB, 128), F32)
    for n in range(wide // 256):
        cols = slice(n * 256, (n + 1) * 256)
        reach = jnp.dot(c_ref[...], state[:, cols], preferred_element_type=F32)
        scale = jnp.dot(full_ref[...], exp_ref[:, cols], preferred_element_type=F32)
        y = y_ref[:, cols] + scale * reach
        buf[:, cols] = y
        y2 = y * y
        squares = squares + y2[:, :128] + y2[:, 128:]
    norm = lax.rsqrt(jnp.sum(squares, axis=1, keepdims=True) * (1.0 / wide) + NORM_EPS)
    for n in range(wide // 256):
        cols = slice(n * 256, (n + 1) * 256)
        out_ref[:, cols] = (buf[:, cols] * norm * gain_ref[:, cols]).astype(BF16)


def place_kernel(slot_ref, got_ref, out_ref):
    out_ref[...] = got_ref[...]


def cost(flops, nbytes):
    return pl.CostEstimate(flops=flops, bytes_accessed=nbytes, transcendentals=0)


def body(conv_input, step_raw, decay_rate, conv_weight, conv_bias, norm_gain, owner_slot):
    seq, ngrp = lax.axis_size("seq"), lax.axis_size("grp")
    place = lax.axis_index("seq")
    width = conv_weight.shape[0]
    rows = conv_input[0]
    length, chans = rows.shape
    heads = step_raw.shape[1]
    per = heads // GROUPS
    d_in = heads * HEAD_DIM
    wide = d_in // GROUPS
    blocks = length // SUB
    slots = owner_slot.shape[0]
    shape = jax.ShapeDtypeStruct

    def along(value, distance):
        return lax.ppermute(value, "seq", [(i, i + distance) for i in range(seq - distance)])

    halo = along(rows[length - HALO :], 1)
    cols_t, rows_q, tail, near, full, shard_log = pl.pallas_call(
        step_kernel,
        out_shape=(
            shape((GROUPS, length, per), F32),
            shape((heads, length), F32),
            shape((length, 2 * heads), BF16),
            shape((length, 2 * heads), BF16),
            shape((length, 2 * heads), BF16),
            shape((heads, 1), F32),
        ),
        cost_estimate=cost(10**7, 10**6),
    )(step_raw[0], decay_rate[:, None])
    shard_log = shard_log[:, 0]
    logs = lax.all_gather(shard_log, "seq", axis=0)

    picks = jnp.arange(2 * heads)[:, None] % heads == jnp.arange(d_in)[None, :] // HEAD_DIM
    expand = picks.astype(BF16)
    bias = conv_bias[None, :]
    b_at, c_at = d_in // STATE, d_in // STATE + GROUPS

    def x_spec(height, moves=False):
        return pl.BlockSpec((height, wide), lambda g, j: (j if moves else 0, g))

    def bc_spec(height, at, moves=False):
        return pl.BlockSpec((height, STATE), lambda g, j: (j if moves else 0, at + g))

    tall = pl.BlockSpec((SUB, 2 * heads), lambda g, j: (j, 0))
    exp_spec = pl.BlockSpec((2 * heads, wide), lambda g, j: (0, g))
    prev_spec = pl.BlockSpec((1, STATE, wide), lambda g, j: (j, 0, g))
    trio = lambda h, m: [x_spec(h, m), bc_spec(h, b_at, m), bc_spec(h, c_at, m)]
    xc, bc, cc, prev, end, end_t = pl.pallas_call(
        state_kernel,
        grid=(GROUPS, blocks),
        in_specs=trio(SUB, True) + trio(HALO, False) + trio(width, False) + trio(1, False)
        + [tall, tall, exp_spec],
        out_specs=[
            x_spec(SUB, True), bc_spec(SUB, 0, True), bc_spec(SUB, 0, True), prev_spec,
            pl.BlockSpec((STATE, wide), lambda g, j: (0, g)),
            pl.BlockSpec((wide, STATE), lambda g, j: (g, 0)),
        ],
        out_shape=(
            shape((length, d_in), BF16),
            shape((length, GROUPS * STATE), BF16),
            shape((length, GROUPS * STATE), BF16),
            shape((blocks, STATE, d_in), BF16),
            shape((STATE, d_in), BF16),
            shape((d_in, STATE), F32),
        ),
        scratch_shapes=[
            pltpu.VMEM((STATE, wide), F32),
            pltpu.VMEM((HALO + SUB, wide), F32),
            pltpu.VMEM((HALO + SUB, STATE), F32),
            pltpu.VMEM((HALO + SUB, STATE), F32),
        ],
        cost_estimate=cost(10**9, 2 * 10**7),
    )(
        rows, rows, rows, halo, halo, halo, conv_weight, conv_weight, conv_weight,
        bias, bias, bias, tail, near, expand,
    )

    got = [along(end, k) for k in range(1, seq)]

    index = jnp.arange(seq)
    after = (index > place)[:, None]
    later = jnp.exp2(jnp.sum(jnp.where(after, logs, 0.0), axis=0))
    sent_state = (end_t.reshape(heads, HEAD_DIM, STATE) * later[:, None, None]).astype(BF16)
    sent_state = sent_state.reshape(ngrp, -1, STATE)
    kept = rows[length - width :].T.reshape(ngrp, -1, STATE)
    kept = jnp.where(place == seq - 1, kept, jnp.zeros_like(kept))
    sent = jnp.concatenate([sent_state, kept], axis=1)
    swapped = lax.all_to_all(sent, "grp", split_axis=0, concat_axis=0, tiled=True)
    tallness = sent.shape[1]
    placed = pl.pallas_call(
        place_kernel,
        grid_spec=pltpu.PrefetchScalarGridSpec(
            num_scalar_prefetch=1,
            grid=(slots,),
            in_specs=[pl.BlockSpec((1, tallness, STATE), lambda i, slot: (i, 0, 0))],
            out_specs=pl.BlockSpec((1, tallness, STATE), lambda i, slot: (slot[i], 0, 0)),
        ),
        out_shape=shape(swapped.shape, BF16),
        cost_estimate=cost(10**6, 2 * 10**6),
    )(owner_slot, swapped)
    summed = lax.psum_scatter(placed, "seq", scatter_dimension=0, tiled=True)
    mine = sent_state.shape[1]
    final_ssm = summed[:, :mine].astype(F32).reshape(slots // seq, heads // ngrp, HEAD_DIM, STATE)
    final_conv = summed[:, mine:].reshape(slots // seq, chans // ngrp, width)

    y = pl.pallas_call(
        intra_kernel,
        grid=(GROUPS, blocks),
        in_specs=[
            x_spec(SUB, True), bc_spec(SUB, 0, True), bc_spec(SUB, 0, True), prev_spec,
            pl.BlockSpec((1, SUB, per), lambda g, j: (g, j, 0)),
            pl.BlockSpec((per, SUB), lambda g, j: (g, j)),
            tall, exp_spec,
        ],
        out_specs=x_spec(SUB, True),
        out_shape=shape((length, d_in), F32),
        cost_estimate=cost(4 * 10**9, 4 * 10**7),
    )(xc, bc, cc, prev, cols_t, rows_q, near, expand)

    coefs = []
    for k in range(1, seq):
        between = ((index > place - k) & (index < place))[:, None]
        coefs.append(jnp.exp2(jnp.sum(jnp.where(between, logs, 0.0), axis=0)))
    coef = jnp.repeat(jnp.stack(coefs), HEAD_DIM, axis=1)
    hops = seq - 1
    mixed = pl.pallas_call(
        functools.partial(norm_kernel, hops),
        grid=(GROUPS, blocks),
        in_specs=[
            x_spec(SUB, True), bc_spec(SUB, 0, True), tall, exp_spec,
            x_spec(hops), x_spec(1),
        ] + [x_spec(STATE)] * hops,
        out_specs=x_spec(SUB, True),
        out_shape=shape((length, d_in), BF16),
        scratch_shapes=[pltpu.VMEM((STATE, wide), BF16), pltpu.VMEM((SUB, wide), F32)],
        cost_estimate=cost(10**9, 2 * 10**7),
    )(y, cc, full, expand, coef, norm_gain[None, :], *got)
    return (mixed[None], final_ssm, final_conv)


def solution(mesh):
    placed = (P("grp", "seq", None), P("grp", None, "seq"), P(), P(), P(), P(), P())
    return jax.shard_map(
        body,
        mesh=mesh,
        in_specs=placed,
        out_specs=(P("grp", "seq", None), P("seq", "grp", None, None), P("seq", "grp", None)),
        check_vma=False,
    )
```

time: 381 us -> 178 us (0.47)
  waiting for transfers between devices: 135 us -> 47.1 us
  other arithmetic: 87.8 us -> 7.06 us
  Pallas kernels: 0 us -> 64.1 us
  local copies, waits for them, and re-layouts: 61.6 us -> 15.3 us
  matrix products: 28.9 us -> 0 us
  blocking collectives: 26.1 us -> 8.93 us
  starting transfers between devices: 25.1 us -> 18 us
    ppermute x4, waiting for transfers between devices: 135 us -> 2.82 us  [along(): lax.ppermute(value, 'seq', [(i, i + distance) for i in range(seq - distan...]
    pallas_call x0 -> x5, Pallas kernels: none -> 64.1 us  [the longest x1 21.9 us: body(): pl.pallas_call(state_kernel, grid=(GROUPS, blocks), in_specs=trio(SUB, Tr...]
    convert_element_type x9 -> x2, other arithmetic: 33.7 us -> 3.21 us  [the longest x1 1.95 us: body(): (end_t.reshape(heads, HEAD_DIM, STATE) * later[:, None, None]).astype(BF16)]
    dot_general x8 -> x0, matrix products: 28.9 us -> none  [the longest x2 13.5 us: block_terms(): jnp.einsum('gktu,ugkp->tgkp', weights, inputs, preferred_element_type=jnp...]
    unnamed x1 -> x2, waiting for transfers between devices: 0.02 us -> 24.9 us
    unnamed x1 -> x0, other arithmetic: 23.4 us -> none
    all_to_all x2 -> x1, waiting for transfers between devices: 0.01 us -> 19.4 us  [body(): lax.all_to_all(sent, 'grp', split_axis=0, concat_axis=0, tiled=True)]
    unnamed x41 -> x12, local copies, waits for them, and re-layouts: 21.2 us -> 5.03 us
  transfers between devices with their start and end apart: 7 -> 6, of which waited for: 3 -> 3; matrix products, arithmetic and copies ran while one was open for 36% -> 7% of each run, Pallas kernels for 0% -> 24%
where the time goes in v1:
time: 178 us; the launch traced here: 176 us
  Pallas kernels  64.1 us (36%)
  waiting for transfers between devices  47.1 us (26%)
  starting transfers between devices  18 us (10%)
  between operations  15.5 us (9%)
  local copies, waits for them, and re-layouts  15.3 us (9%)
  blocking collectives  8.93 us (5%)
  other arithmetic  7.06 us (4%)
    unnamed x2, waiting for transfers between devices  24.9 us
    pallas_call x1, Pallas kernels, body(): pl.pallas_call(state_kernel, grid=(GROUPS, blocks), in_specs=trio(SUB, Tr...  21.9 us
    all_to_all x1, waiting for transfers between devices, body(): lax.all_to_all(sent, 'grp', split_axis=0, concat_axis=0, tiled=True)  19.4 us
    pallas_call x1, Pallas kernels, body(): pl.pallas_call(intra_kernel, grid=(GROUPS, blocks), in_specs=[x_spec(SUB,...  17.1 us
    pallas_call x1, Pallas kernels, body(): pl.pallas_call(functools.partial(norm_kernel, hops), grid=(GROUPS, blocks...  16.2 us
    ppermute x4, starting transfers between devices, along(): lax.ppermute(value, 'seq', [(i, i + distance) for i in range(seq - distan...  13.1 us
    unnamed x1, blocking collectives  8.93 us
    pallas_call x1, Pallas kernels, body(): pl.pallas_call(place_kernel, grid_spec=pltpu.PrefetchScalarGridSpec(num_s...  5.87 us
  transfers between devices with their start and end apart: 6, of which 3 were waited for; matrix products, arithmetic and copies ran while one was open for 7% of the time, Pallas kernels for 24%

profile of v1, /device:TPU:0, one launch (start us, length us, event | category | flops | bytes accessed | tf_op | source)
XLA Modules:
  0.0 176.0 jit_solution(8691106859147518407)
XLA Ops:
  7.2 0.9 slice_bitcast_fusion
  8.1 4.9 %collective-permute-start = (bf16[8,5120]{1,0:T(8,128)(2,1)S(1)}, bf16[8,5120]{1,0:T(8,128)(2,1)S(1)}, u32[]{:S(2)}, u32[]{:S(2)}) collective-permute-start(bf16[8,5120]{1,0:T(8,128)(2,1)S(1)} %slice_bitcast_fusion), channel_id=1, source_target_pairs={{0,8},{8,16},{16,24},{1,9},{9,17},{17,25},{2,10},{10,18},{18,26},{... | collective-permute-start | bytes 245768 | tf_op jit(solution)/shard_map/ppermute | solution.py:184
  13.0 1.4 copy.19.rate_ref
  14.3 3.0 %shard_map.94 = (f32[4,512,16]{2,1,0:T(8,128)}, f32[64,512]{1,0:T(8,128)}, bf16[512,128]{1,0:T(8,128)(2,1)}, bf16[512,128]{1,0:T(8,128)(2,1)}, bf16[512,128]{1,0:T(8,128)(2,1)}, /*index=5*/f32[64,1]{1,0:T(8,128)}) custom-call(f32[64,512]{1,0:T(8,128)} %bitcast.28, f32[64,1]{1,0:T(8,128)} %copy.19.rate_ref), custom_call_target="tpu_custom_call" | custom-call | flops 10000000 | bytes 1000000 | tf_op jit(solution)/shard_map/pallas_call | solution.py:187
  17.4 0.9 reduce
  18.3 1.3 fusion.3
  20.2 0.2 dynamic-update-slice
  20.5 8.9 %all-reduce = f32[256]{0:T(256)S(1)} all-reduce(f32[256]{0:T(256)S(1)} %dynamic-update-slice), channel_id=2, replica_groups=mesh['seq'=4,'grp'=8] {'seq'}, use_global_device_ids=true, to_apply=%add | all-reduce | flops 256 | bytes 2048
  29.4 0.1 reshape.165
  29.5 0.9 select_bitcast_fusion
  30.4 1.3 compare_convert_fusion.exp_ref
  31.7 0.1 select_reduce_fusion
  31.8 1.3 broadcast_in_dim.55.bx_ref.bb_ref.bc_ref
  33.1 0.6 copy.20
  33.7 2.5 %select_n.70 = bf16[8,20,128]{2,1,0:T(8,128)(2,1)S(1)} reshape(bf16[5120,4]{1,0:T(8,128)(2,1)S(1)} %copy.20) | data formatting | bytes 81920 | tf_op jit(solution)/shard_map/jit(_where)/select_n | solution.py:255
  36.3 0.1 exp2.101
  36.3 0.1 mul.13
  36.4 0.1 mul.14
  36.5 0.0 collective-permute-done.hx_ref.hb_ref.hc_ref
  36.5 0.0 copy-start.3
  36.5 0.6 copy-done.3
  37.1 21.9 %shard_map.95 = (bf16[512,4096]{1,0:T(8,128)(2,1)}, bf16[512,512]{1,0:T(8,128)(2,1)}, bf16[512,512]{1,0:T(8,128)(2,1)}, bf16[4,128,4096]{2,1,0:T(8,128)(2,1)}, b...) custom-call(bf16[512,5120]{1,0:T(8,128)(2,1)} %bitcast.22, bf16[512,5120]{1,0:T(8,128)(2,1)} %bitcast.23, ...), custom_call_target="tpu_custom_call" | custom-call | flops 1000000000 | bytes 20000000 | tf_op jit(solution)/shard_map/pallas_call | solution.py:217
  59.1 1.9 %multiply_convert_fusion = bf16[8,512,128]{2,1,0:T(8,128)(2,1)S(1)} fusion(f32[8,512,128]{2,1,0:T(8,128)} %bitcast.26, f32[8,512]{1,0:T(8,128)S(1)} %mul.14), kind=kLoop, calls=%fused_computation | loop fusion | flops 1048576 | bytes 3162112 | tf_op jit(solution)/shard_map/convert_element_type | solution.py:252
  61.0 1.1 pad_maximum_fusion
  62.1 4.9 %all-to-all-start = ((bf16[8,532,128]{2,1,0:T(8,128)(2,1)}), bf16[8,532,128]{2,1,0:T(8,128)(2,1)S(1)}, u32[]{:S(2)}, u32[]{:S(2)}) async-start(bf16[8,532,128]{2,1,0:T(8,128)(2,1)} %pad_maximum_fusion), calls=%async_computation | async-start | bytes 2195456 | tf_op jit(solution)/shard_map/all_to_all | solution.py:257
  67.0 0.0 all-reduce.4.cloned.1.call-start
  67.0 2.6 %collective-permute-start.1 = (bf16[128,4096]{1,0:T(8,128)(2,1)}, bf16[128,4096]{1,0:T(8,128)(2,1)S(1)}, u32[]{:S(2)}, u32[]{:S(2)}) collective-permute-start(bf16[128,4096]{1,0:T(8,128)(2,1)} %get-tuple-element.25), channel_id=1, source_target_pairs={{0,8},{8,16},{16,24},{1,9},{9,17},{17,25},{2,10},{10,18},{18,26},{... | collective-permute-start | bytes 3145736 | tf_op jit(solution)/shard_map/ppermute | solution.py:184
  69.6 3.3 %collective-permute-start.2 = (bf16[128,4096]{1,0:T(8,128)(2,1)}, bf16[128,4096]{1,0:T(8,128)(2,1)S(1)}, u32[]{:S(2)}, u32[]{:S(2)}) collective-permute-start(bf16[128,4096]{1,0:T(8,128)(2,1)} %get-tuple-element.25), channel_id=1, source_target_pairs={{0,16},{8,24},{1,17},{9,25},{2,18},{10,26},{3,19},{11,27},{4,20},{... | collective-permute-start | bytes 3145736 | tf_op jit(solution)/shard_map/ppermute | solution.py:184
  72.9 2.3 %collective-permute-start.3 = (bf16[128,4096]{1,0:T(8,128)(2,1)}, bf16[128,4096]{1,0:T(8,128)(2,1)}, u32[]{:S(2)}, u32[]{:S(2)}) collective-permute-start(bf16[128,4096]{1,0:T(8,128)(2,1)} %get-tuple-element.25), channel_id=1, source_target_pairs={{0,24},{1,25},{2,26},{3,27},{4,28},{5,29},{6,30},{7,31}} | collective-permute-start | bytes 3145736 | tf_op jit(solution)/shard_map/ppermute | solution.py:184
  75.3 19.4 %all-to-all-done.got_ref = bf16[8,532,128]{2,1,0:T(8,128)(2,1)S(1)} async-done(((bf16[8,532,128]{2,1,0:T(8,128)(2,1)}), bf16[8,532,128]{2,1,0:T(8,128)(2,1)S(1)}, u32[]{:S(2)}, u32[]{:S(2)}) %all-to-all-start) | async-done | bytes 1089568 | tf_op jit(solution)/shard_map/all_to_all | solution.py:257
  94.6 0.0 copy-start
  94.6 1.0 copy-done
  95.6 5.9 %shard_map.98 = bf16[8,532,128]{2,1,0:T(8,128)(2,1)} custom-call(s32[8]{0:T(128)} %slot_ref.1, bf16[8,532,128]{2,1,0:T(8,128)(2,1)} %copy-done), custom_call_target="tpu_custom_call" | custom-call | flops 1000000 | bytes 2000000 | tf_op jit(solution)/shard_map/pallas_call | solution.py:259
  101.5 0.0 all-reduce.4.cloned.1.call-update
  101.5 0.1 broadcast_in_dim.61
  101.6 0.7 reshape.158.coef_ref
  103.0 17.1 %shard_map.96.y_ref = f32[512,4096]{1,0:T(8,128)} custom-call(bf16[512,4096]{1,0:T(8,128)(2,1)} %get-tuple-element.17.x_ref, bf16[512,512]{1,0:T(8,128)(2,1)} %get-tuple-element.18.b_ref, bf16[512,512]{1,0:T(8,128)(2,1)} %get-tuple-element.19.c_ref, bf16[4,128,4096]{2,1,0:T(8,128)(2,1)} %get-tuple-element.20.prev_ref, ...), custom_call_target="tpu_custom_call" | custom-call | flops 4000000000 | bytes 40000000 | tf_op jit(solution)/shard_map/pallas_call | solution.py:275
  120.1 0.0 collective-permute-done.1.rest_0_
  120.1 0.0 copy-start.1
  120.1 2.8 %collective-permute-done.2.rest_1_ = bf16[128,4096]{1,0:T(8,128)(2,1)S(1)} collective-permute-done((bf16[128,4096]{1,0:T(8,128)(2,1)}, bf16[128,4096]{1,0:T(8,128)(2,1)S(1)}, u32[]{:S(2)}, u32[]{:S(2)}) %collective-permute-start.2) | collective-permute-done | bytes 1048608 | tf_op jit(solution)/shard_map/ppermute | solution.py:184
  122.9 0.0 copy-start.2
  122.9 0.0 collective-permute-done.3.rest_2_
  122.9 0.0 copy-done.1
  122.9 1.1 copy-done.2
  124.0 16.2 %shard_map.97 = bf16[512,4096]{1,0:T(8,128)(2,1)} custom-call(f32[512,4096]{1,0:T(8,128)} %shard_map.96.y_ref, bf16[512,512]{1,0:T(8,128)(2,1)} %get-tuple-element.19.c_ref, bf16[512,128]{1,0:T(8,128)(2,1)} %get-tuple-element.23.full_ref, bf16[128,4096]{1,0:T(8,128)(2,1)} %compare_convert_fusion.exp_ref, f32[3,4096]{1,0:T(4,128)} %reshape.158.coef_ref, ...), custom_call_target="tpu_custom_call" | custom-call | flops 1000000000 | bytes 20000000 | tf_op jit(solution)/shard_map/pallas_call | solution.py:295
  140.2 24.9 %all-reduce.4.cloned.1.call-done = bf16[8,532,128]{2,1,0:T(8,128)(2,1)} async-done(((bf16[8,532,128]{2,1,0:T(8,128)(2,1)}), bf16[8,532,128]{2,1,0:T(8,128)(2,1)}) %all-reduce.4.cloned.1.call-update) | async-done | bytes 1089552
  165.1 1.0 constant_dynamic-slice_fusion
  166.1 0.8 convert.1
  166.9 0.7 constant_dynamic-slice_fusion.1
  167.6 0.7 reshape.162
  168.4 0.8 copy.21
  (10 shorter events, 0.1 us)
Async XLA Ops:
  8.1 28.4 %collective-permute-start = (bf16[8,5120]{1,0:T(8,128)(2,1)S(1)}, bf16[8,5120]{1,0:T(8,128)(2,1)S(1)}, u32[]{:S(2)}, u32[]{:S(2)}) collective-permute-start(bf16[8,5120]{1,0:T(8,128)(2,1)S(1)} %slice_bitcast_fusion), channel_id=1, source_target_pairs={{0,8},{8,16},{16,24},{1,9},{9,17},{17,25},{2,10},{10,18},{18,26},{... | collective-permute-start | bytes 245768 | tf_op jit(solution)/shard_map/ppermute | solution.py:184
  36.5 0.6 copy-start.3
  62.1 32.5 %all-to-all-start = ((bf16[8,532,128]{2,1,0:T(8,128)(2,1)}), bf16[8,532,128]{2,1,0:T(8,128)(2,1)S(1)}, u32[]{:S(2)}, u32[]{:S(2)}) async-start(bf16[8,532,128]{2,1,0:T(8,128)(2,1)} %pad_maximum_fusion), calls=%async_computation | async-start | bytes 2195456 | tf_op jit(solution)/shard_map/all_to_all | solution.py:257
  67.0 98.1 %all-reduce.4.cloned.1.call-start = ((), (), s32[]{:S(2)}) async-start(), calls=%async_computation.1 | async-start | bytes 2195456
  67.0 53.0 %collective-permute-start.1 = (bf16[128,4096]{1,0:T(8,128)(2,1)}, bf16[128,4096]{1,0:T(8,128)(2,1)S(1)}, u32[]{:S(2)}, u32[]{:S(2)}) collective-permute-start(bf16[128,4096]{1,0:T(8,128)(2,1)} %get-tuple-element.25), channel_id=1, source_target_pairs={{0,8},{8,16},{16,24},{1,9},{9,17},{17,25},{2,10},{10,18},{18,26},{... | collective-permute-start | bytes 3145736 | tf_op jit(solution)/shard_map/ppermute | solution.py:184
  69.6 53.3 %collective-permute-start.2 = (bf16[128,4096]{1,0:T(8,128)(2,1)}, bf16[128,4096]{1,0:T(8,128)(2,1)S(1)}, u32[]{:S(2)}, u32[]{:S(2)}) collective-permute-start(bf16[128,4096]{1,0:T(8,128)(2,1)} %get-tuple-element.25), channel_id=1, source_target_pairs={{0,16},{8,24},{1,17},{9,25},{2,18},{10,26},{3,19},{11,27},{4,20},{... | collective-permute-start | bytes 3145736 | tf_op jit(solution)/shard_map/ppermute | solution.py:184
  72.9 50.0 %collective-permute-start.3 = (bf16[128,4096]{1,0:T(8,128)(2,1)}, bf16[128,4096]{1,0:T(8,128)(2,1)}, u32[]{:S(2)}, u32[]{:S(2)}) collective-permute-start(bf16[128,4096]{1,0:T(8,128)(2,1)} %get-tuple-element.25), channel_id=1, source_target_pairs={{0,24},{1,25},{2,26},{3,27},{4,28},{5,29},{6,30},{7,31}} | collective-permute-start | bytes 3145736 | tf_op jit(solution)/shard_map/ppermute | solution.py:184
  94.6 1.0 copy-start
  120.1 2.8 %copy-start.1 = (bf16[128,4096]{1,0:T(8,128)(2,1)}, bf16[128,4096]{1,0:T(8,128)(2,1)S(1)}, u32[]{:S(2)}) copy-start(bf16[128,4096]{1,0:T(8,128)(2,1)S(1)} %collective-permute-done.1.rest_0_) | copy-start | bytes 3145732
  122.9 1.1 copy-start.2
Sparse Core Ops, SparseCore 0:
  101.6 63.4 all-reduce.3

commit v2 on v1

v2 whole, which is shorter than its diff:
```python
import functools
import math

import jax
import jax.numpy as jnp
from jax import lax
from jax.experimental import pallas as pl
from jax.experimental.pallas import tpu as pltpu
from jax.sharding import PartitionSpec as P

HEAD_DIM = 64
STATE = 128
GROUPS = 4
SUB = 128
HALO = 8
LOG_ROWS = 16
NORM_EPS = 1.0
LOG2E = math.log2(math.e)
F32 = jnp.float32
BF16 = jnp.bfloat16
NEG = -1e30


def split_rows(value):
    high = value.astype(BF16).astype(F32)
    return jnp.concatenate([high, value - high], axis=0).T.astype(BF16)


def step_kernel(raw_ref, rate_ref, col_ref, row_ref, tail_ref, near_ref, full_ref, log_ref):
    heads, length = raw_ref.shape
    per = heads // GROUPS
    u = lax.broadcasted_iota(jnp.int32, (SUB, SUB), 0)
    t = lax.broadcasted_iota(jnp.int32, (SUB, SUB), 1)
    upper = jnp.where(u <= t, 1.0, 0.0).astype(F32)
    base = jnp.zeros((heads, 1), F32)
    log = jnp.zeros((1, heads), F32)
    for j in range(length // SUB):
        cut = slice(j * SUB, (j + 1) * SUB)
        raw = raw_ref[:, cut]
        dt = jnp.maximum(raw, 0.0) + jnp.log(1.0 + jnp.exp(-jnp.abs(raw)))
        rate = dt * (rate_ref[...] * -LOG2E)
        cs = jnp.dot(rate, upper, precision=lax.Precision.HIGHEST, preferred_element_type=F32)
        q = cs - jnp.log(dt) * LOG2E
        row_ref[:, cut] = q
        total = cs[:, SUB - 1 :]
        turned = cs.T
        for g in range(GROUPS):
            col_ref[g, cut, :] = turned[:, g * per : (g + 1) * per]
        tail_ref[cut, :] = split_rows(jnp.exp2(total - q))
        near_ref[cut, :] = split_rows(jnp.exp2(cs))
        full_ref[cut, :] = split_rows(jnp.exp2(cs + base))
        base = base + total
        log = log + turned[SUB - 1 :, :]
    terms = []
    for _ in range(3):
        high = log.astype(BF16).astype(F32)
        terms.append(high)
        log = log - high
    terms.append(jnp.zeros((LOG_ROWS - 3, heads), F32))
    terms = jnp.concatenate(terms, axis=0)
    log_ref[...] = jnp.concatenate([terms, jnp.zeros_like(terms)], axis=1).astype(BF16)


def conv_silu(buf, w_ref, b_ref, cols, row):
    total = b_ref[:, cols].astype(F32)
    width = w_ref.shape[0]
    for k in range(width):
        start = row + HALO - width + 1 + k
        total = total + w_ref[k : k + 1, cols].astype(F32) * buf[start : start + SUB, cols]
    half = 0.5 * total
    return half + half * jnp.tanh(half)


def state_kernel(
    x_ref, b_ref, c_ref, hx_ref, hb_ref, hc_ref, wx_ref, wb_ref, wc_ref, bx_ref, bb_ref, bc_ref,
    tail_ref, near_ref, log_ref, exp_ref, xo_ref, bo_ref, co_ref, prev_ref, end_ref, endt_ref,
    turned, xbuf, bbuf, cbuf,
):
    length, wide = x_ref.shape
    blocks = length // SUB
    for buf, ref, h_ref in ((bbuf, b_ref, hb_ref), (cbuf, c_ref, hc_ref)):
        buf[:HALO, :] = h_ref[...].astype(F32)
        buf[HALO:, :] = ref[...].astype(F32)
    whole = slice(0, STATE)
    for j in range(blocks):
        cut = slice(j * SUB, (j + 1) * SUB)
        b = conv_silu(bbuf, wb_ref, bb_ref, whole, j * SUB)
        bo_ref[cut, :] = b.astype(BF16)
        turned[j] = b.T.astype(BF16)
        co_ref[cut, :] = conv_silu(cbuf, wc_ref, bc_ref, whole, j * SUB).astype(BF16)

    for n in range(wide // 256):
        cols = slice(n * 256, (n + 1) * 256)
        xbuf[:HALO, :] = hx_ref[:, cols].astype(F32)
        xbuf[HALO:, :] = x_ref[:, cols].astype(F32)
        expand = exp_ref[:, cols]
        state = jnp.zeros((STATE, 256), F32)
        for j in range(blocks):
            cut = slice(j * SUB, (j + 1) * SUB)
            tail = jnp.dot(tail_ref[cut, :], expand, preferred_element_type=F32)
            ends = near_ref[(j + 1) * SUB - 16 : (j + 1) * SUB, :]
            decay = jnp.dot(ends, expand, preferred_element_type=F32)[15:16, :]
            for m in range(2):
                part = slice(n * 256 + m * 128, n * 256 + (m + 1) * 128)
                here = slice(m * 128, (m + 1) * 128)
                total = bx_ref[:, part].astype(F32)
                for k in range(wx_ref.shape[0]):
                    start = j * SUB + HALO - wx_ref.shape[0] + 1 + k
                    total = total + wx_ref[k : k + 1, part].astype(F32) * xbuf[start : start + SUB, here]
                half = 0.5 * total
                xo_ref[cut, part] = (half + half * jnp.tanh(half)).astype(BF16)
            scaled = (xo_ref[cut, cols].astype(F32) * tail).astype(BF16)
            local = jnp.dot(turned[j], scaled, preferred_element_type=F32)
            prev_ref[j, :, cols] = state.astype(BF16)
            state = decay * state + local
        end_ref[:STATE, cols] = state.astype(BF16)
        end_ref[STATE:, cols] = jnp.dot(log_ref[...], expand, preferred_element_type=F32).astype(BF16)
        for m in range(2):
            part = slice(n * 256 + m * 128, n * 256 + (m + 1) * 128)
            endt_ref[part, :] = state[:, m * 128 : (m + 1) * 128].T.astype(BF16)


def intra_kernel(x_ref, b_ref, c_ref, prev_ref, col_ref, row_ref, near_ref, exp_ref, y_ref):
    b, c = b_ref[...], c_ref[...]
    scores = lax.dot_general(c, b, (((1,), (1,)), ((), ())), preferred_element_type=F32)
    t = lax.broadcasted_iota(jnp.int32, (SUB, SUB), 0)
    u = lax.broadcasted_iota(jnp.int32, (SUB, SUB), 1)
    causal = u <= t
    low = lax.broadcasted_iota(jnp.int32, (SUB, 2 * HEAD_DIM), 1) < HEAD_DIM
    zero = jnp.zeros((SUB, 2 * HEAD_DIM), BF16)
    wide = x_ref.shape[1]
    for n in range(wide // (2 * HEAD_DIM)):
        cols = slice(n * 128, (n + 1) * 128)
        parts = []
        for k in (2 * n, 2 * n + 1):
            gap = col_ref[0, :, k : k + 1] - row_ref[k : k + 1, :]
            parts.append((jnp.exp2(jnp.where(causal, gap, NEG)) * scores).astype(BF16))
        x = x_ref[:, cols]
        pair = jnp.concatenate([jnp.where(low, x, zero), jnp.where(low, zero, x)], axis=0)
        weights = jnp.concatenate(parts, axis=1)
        y = jnp.dot(weights, pair, preferred_element_type=F32)
        reach = jnp.dot(c, prev_ref[0, :, cols], preferred_element_type=F32)
        near = jnp.dot(near_ref[...], exp_ref[:, cols], preferred_element_type=F32)
        y_ref[:, cols] = y + near * reach


def norm_kernel(hops, y_ref, c_ref, full_ref, exp_ref, gain_ref, *rest):
    got, out_ref, state, buf, squares = rest[:hops], rest[hops], *rest[hops + 1 :]
    length, wide = y_ref.shape

    def log_of(ref):
        rows = ref[STATE:, :].astype(F32)
        return rows[0:1, :] + rows[1:2, :] + rows[2:3, :]

    total = got[0][:STATE, :].astype(F32)
    since = log_of(got[0])
    for k in range(1, hops):
        total = total + jnp.exp2(since) * got[k][:STATE, :].astype(F32)
        since = since + log_of(got[k])
    state[...] = total.astype(BF16)

    for n in range(wide // 256):
        cols = slice(n * 256, (n + 1) * 256)
        reach = jnp.dot(c_ref[...], state[:, cols], preferred_element_type=F32)
        scale = jnp.dot(full_ref[...], exp_ref[:, cols], preferred_element_type=F32)
        y = y_ref[:, cols] + scale * reach
        buf[:, cols] = y
        y2 = y * y
        more = y2[:, :128] + y2[:, 128:]
        squares[...] = more if n == 0 else squares[...] + more
    for t in range(length // SUB):
        cut = slice(t * SUB, (t + 1) * SUB)
        mean = jnp.sum(squares[cut, :], axis=1, keepdims=True) * (1.0 / wide)
        norm = lax.rsqrt(mean + NORM_EPS)
        for n in range(wide // 128):
            cols = slice(n * 128, (n + 1) * 128)
            out_ref[cut, cols] = (buf[cut, cols] * norm * gain_ref[:, cols]).astype(BF16)


def place_kernel(slot_ref, got_ref, out_ref):
    out_ref[...] = got_ref[...]


def cost(flops, nbytes):
    return pl.CostEstimate(flops=flops, bytes_accessed=nbytes, transcendentals=0)


def body(conv_input, step_raw, decay_rate, conv_weight, conv_bias, norm_gain, owner_slot):
    seq, ngrp = lax.axis_size("seq"), lax.axis_size("grp")
    place = lax.axis_index("seq")
    width = conv_weight.shape[0]
    rows = conv_input[0]
    length, chans = rows.shape
    heads = step_raw.shape[1]
    per = heads // GROUPS
    d_in = heads * HEAD_DIM
    wide = d_in // GROUPS
    blocks = length // SUB
    slots = owner_slot.shape[0]
    shape = jax.ShapeDtypeStruct

    def along(value, distance):
        return lax.ppermute(value, "seq", [(i, i + distance) for i in range(seq - distance)])

    halo = along(rows[length - HALO :], 1)
    cols_t, rows_q, tail, near, full, shard_log = pl.pallas_call(
        step_kernel,
        out_shape=(
            shape((GROUPS, length, per), F32),
            shape((heads, length), F32),
            shape((length, 2 * heads), BF16),
            shape((length, 2 * heads), BF16),
            shape((length, 2 * heads), BF16),
            shape((LOG_ROWS, 2 * heads), BF16),
        ),
        cost_estimate=cost(10**7, 10**6),
    )(step_raw[0], decay_rate[:, None])

    picks = jnp.arange(2 * heads)[:, None] % heads == jnp.arange(d_in)[None, :] // HEAD_DIM
    expand = picks.astype(BF16)
    bias = conv_bias[None, :]
    b_at, c_at = d_in // STATE, d_in // STATE + GROUPS

    def x_spec(height, moves=False):
        return pl.BlockSpec((height, wide), lambda g, j: (j if moves else 0, g))

    def bc_spec(height, at, moves=False):
        return pl.BlockSpec((height, STATE), lambda g, j: (j if moves else 0, at + g))

    tall = pl.BlockSpec((SUB, 2 * heads), lambda g, j: (j, 0))
    exp_spec = pl.BlockSpec((2 * heads, wide), lambda g, j: (0, g))
    prev_spec = pl.BlockSpec((1, STATE, wide), lambda g, j: (j, 0, g))
    strip = lambda height: pl.BlockSpec((height, wide), lambda g: (0, g))
    thin = lambda height, at: pl.BlockSpec((height, STATE), lambda g: (0, at + g))
    flat = lambda height: pl.BlockSpec((height, 2 * heads), lambda g: (0, 0))
    trio = lambda h: [strip(h), thin(h, b_at), thin(h, c_at)]
    xc, bc, cc, prev, end, end_t = pl.pallas_call(
        state_kernel,
        grid=(GROUPS,),
        in_specs=trio(length) + trio(HALO) + trio(width) + trio(1)
        + [flat(length), flat(length), flat(LOG_ROWS), strip(2 * heads)],
        out_specs=[
            strip(length), thin(length, 0), thin(length, 0),
            pl.BlockSpec((blocks, STATE, wide), lambda g: (0, 0, g)),
            strip(STATE + LOG_ROWS),
            pl.BlockSpec((wide, STATE), lambda g: (g, 0)),
        ],
        out_shape=(
            shape((length, d_in), BF16),
            shape((length, GROUPS * STATE), BF16),
            shape((length, GROUPS * STATE), BF16),
            shape((blocks, STATE, d_in), BF16),
            shape((STATE + LOG_ROWS, d_in), BF16),
            shape((d_in, STATE), BF16),
        ),
        scratch_shapes=[
            pltpu.VMEM((blocks, STATE, SUB), BF16),
            pltpu.VMEM((HALO + length, 256), F32),
            pltpu.VMEM((HALO + length, STATE), F32),
            pltpu.VMEM((HALO + length, STATE), F32),
        ],
        cost_estimate=cost(10**9, 2 * 10**7),
    )(
        rows, rows, rows, halo, halo, halo, conv_weight, conv_weight, conv_weight,
        bias, bias, bias, tail, near, shard_log, expand,
    )

    got = [along(end, k) for k in range(1, seq)]

    sent_state = end_t.reshape(ngrp, -1, STATE)
    kept = rows[length - width :].T.reshape(ngrp, -1, STATE)
    log_terms = shard_log[:, :heads].reshape(LOG_ROWS, ngrp, -1).swapaxes(0, 1)
    log_terms = jnp.pad(log_terms, ((0, 0), (0, 0), (0, STATE - log_terms.shape[2])))
    sent = jnp.concatenate([sent_state, kept, log_terms], axis=1)
    swapped = lax.all_to_all(sent, "grp", split_axis=0, concat_axis=0, tiled=True)

    y = pl.pallas_call(
        intra_kernel,
        grid=(GROUPS, blocks),
        in_specs=[
            x_spec(SUB, True), bc_spec(SUB, 0, True), bc_spec(SUB, 0, True), prev_spec,
            pl.BlockSpec((1, SUB, per), lambda g, j: (g, j, 0)),
            pl.BlockSpec((per, SUB), lambda g, j: (g, j)),
            tall, exp_spec,
        ],
        out_specs=x_spec(SUB, True),
        out_shape=shape((length, d_in), F32),
        cost_estimate=cost(4 * 10**9, 4 * 10**7),
    )(xc, bc, cc, prev, cols_t, rows_q, near, expand)

    swapped, y = lax.optimization_barrier((swapped, y))
    tallness = sent.shape[1]
    placed = pl.pallas_call(
        place_kernel,
        grid_spec=pltpu.PrefetchScalarGridSpec(
            num_scalar_prefetch=1,
            grid=(slots,),
            in_specs=[pl.BlockSpec((1, tallness, STATE), lambda i, slot: (i, 0, 0))],
            out_specs=pl.BlockSpec((1, tallness, STATE), lambda i, slot: (slot[i], 0, 0)),
        ),
        out_shape=shape(swapped.shape, BF16),
        cost_estimate=cost(10**6, 2 * 10**6),
    )(owner_slot, swapped)
    owned = lax.all_to_all(placed, "seq", split_axis=0, concat_axis=0, tiled=True)

    hops = seq - 1
    mixed = pl.pallas_call(
        functools.partial(norm_kernel, hops),
        grid=(GROUPS,),
        in_specs=[strip(length), thin(length, 0), flat(length), strip(2 * heads), strip(1)]
        + [strip(STATE + LOG_ROWS)] * hops,
        out_specs=strip(length),
        out_shape=shape((length, d_in), BF16),
        scratch_shapes=[
            pltpu.VMEM((STATE, wide), BF16),
            pltpu.VMEM((length, wide), F32),
            pltpu.VMEM((length, 128), F32),
        ],
        cost_estimate=cost(10**9, 2 * 10**7),
    )(y, cc, full, expand, norm_gain[None, :], *got)

    owned, mixed = lax.optimization_barrier((owned, mixed))
    mine, each = sent_state.shape[1], heads // ngrp
    owned = owned.reshape(seq, slots // seq, tallness, STATE)
    logs = jnp.sum(owned[:, :, -LOG_ROWS : 3 - LOG_ROWS, :each].astype(F32), axis=2)
    index = jnp.arange(seq)
    after = (index[None, :] > index[:, None]).astype(F32)
    weight = jnp.exp2(jnp.sum(after[:, :, None, None] * logs[None], axis=1))
    states = owned[:, :, :mine].reshape(seq, slots // seq, each, HEAD_DIM, STATE)
    final_ssm = jnp.sum(weight[..., None, None] * states.astype(F32), axis=0)
    final_conv = owned[seq - 1, :, mine:-LOG_ROWS].reshape(slots // seq, chans // ngrp, width)
    return (mixed[None], final_ssm, final_conv)


def solution(mesh):
    placed = (P("grp", "seq", None), P("grp", None, "seq"), P(), P(), P(), P(), P())
    return jax.shard_map(
        body,
        mesh=mesh,
        in_specs=placed,
        out_specs=(P("grp", "seq", None), P("seq", "grp", None, None), P("seq", "grp", None)),
        check_vma=False,
    )
```

time: 178 us -> 122 us (0.69)
  waiting for transfers between devices: 47.1 us -> 26.7 us
  between operations: 15.5 us -> 0.77 us
  Pallas kernels: 64.1 us -> 54.1 us
  blocking collectives: 8.93 us -> 0 us
  starting transfers between devices: 18 us -> 21 us
  local copies, waits for them, and re-layouts: 15.3 us -> 12.8 us
  other arithmetic: 7.06 us -> 5.26 us
    unnamed x2 -> x0, waiting for transfers between devices: 24.9 us -> none
    ppermute x4, waiting for transfers between devices: 2.82 us -> 23.1 us  [along(): lax.ppermute(value, 'seq', [(i, i + distance) for i in range(seq - distan...]
    all_to_all x1, waiting for transfers between devices: 19.4 us -> 3.56 us  [body(): lax.all_to_all(sent, 'grp', split_axis=0, concat_axis=0, tiled=True)]
    pallas_call x2, Pallas kernels: 38.2 us -> 28.3 us  [the longest x1 18.8 us: body(): pl.pallas_call(state_kernel, grid=(GROUPS,), in_specs=trio(length) + trio...]
    unnamed x1 -> x0, blocking collectives: 8.93 us -> none
    all_to_all x0 -> x1, starting transfers between devices: none -> 3.52 us  [body(): lax.all_to_all(placed, 'seq', split_axis=0, concat_axis=0, tiled=True)]
    select_n x2 -> x0, local copies, waits for them, and re-layouts: 3.13 us -> none  [body(): kept = jnp.where(place == seq - 1, kept, jnp.zeros_like(kept))]
    convert_element_type x1, other arithmetic: 1.95 us -> 0.01 us  [body(): after = (index[None, :] > index[:, None]).astype(F32)]
  transfers between devices with their start and end apart: 6 -> 6, of which waited for: 3 -> 2; matrix products, arithmetic and copies ran while one was open for 7% -> 7% of each run, Pallas kernels for 24% -> 29%
where the time goes in v2:
time: 122 us; the launch traced here: 121 us
  Pallas kernels  54.1 us (44%)
  waiting for transfers between devices  26.7 us (22%)
  starting transfers between devices  21 us (17%)
  local copies, waits for them, and re-layouts  12.8 us (10%)
  other arithmetic  5.26 us (4%)
    ppermute x4, waiting for transfers between devices, along(): lax.ppermute(value, 'seq', [(i, i + distance) for i in range(seq - distan...  23.1 us
    pallas_call x1, Pallas kernels, body(): pl.pallas_call(state_kernel, grid=(GROUPS,), in_specs=trio(length) + trio...  18.8 us
    pallas_call x1, Pallas kernels, body(): pl.pallas_call(intra_kernel, grid=(GROUPS, blocks), in_specs=[x_spec(SUB,...  17 us
    ppermute x4, starting transfers between devices, along(): lax.ppermute(value, 'seq', [(i, i + distance) for i in range(seq - distan...  12.6 us
    pallas_call x1, Pallas kernels, body(): pl.pallas_call(functools.partial(norm_kernel, hops), grid=(GROUPS,), in_s...  9.53 us
    pallas_call x1, Pallas kernels, body(): pl.pallas_call(place_kernel, grid_spec=pltpu.PrefetchScalarGridSpec(num_s...  5.89 us
    all_to_all x1, starting transfers between devices, body(): lax.all_to_all(sent, 'grp', split_axis=0, concat_axis=0, tiled=True)  4.88 us
    all_to_all x1, waiting for transfers between devices, body(): lax.all_to_all(sent, 'grp', split_axis=0, concat_axis=0, tiled=True)  3.56 us
  transfers between devices with their start and end apart: 6, of which 2 were waited for; matrix products, arithmetic and copies ran while one was open for 7% of the time, Pallas kernels for 29%

profile of v2, /device:TPU:0, one launch (start us, length us, event | category | flops | bytes accessed | tf_op | source)
XLA Modules:
  0.0 120.6 jit_solution(13989218479902381587)
XLA Ops:
  0.6 0.9 slice_bitcast_fusion
  1.5 4.9 %collective-permute-start = (bf16[8,5120]{1,0:T(8,128)(2,1)S(1)}, bf16[8,5120]{1,0:T(8,128)(2,1)S(1)}, u32[]{:S(2)}, u32[]{:S(2)}) collective-permute-start(bf16[8,5120]{1,0:T(8,128)(2,1)S(1)} %slice_bitcast_fusion), channel_id=1, source_target_pairs={{0,8},{8,16},{16,24},{1,9},{9,17},{17,25},{2,10},{10,18},{18,26},{... | collective-permute-start | bytes 245768 | tf_op jit(solution)/shard_map/ppermute | solution.py:203
  6.4 0.9 slice_bitcast_fusion.1
  7.3 1.2 %compare_convert_fusion.exp_ref = bf16[128,4096]{1,0:T(8,128)(2,1)} fusion(s32[4096]{0:T(1024)S(1)} %add_select_fusion, s32[128]{0:T(128)S(1)} %and_select_fusion), kind=kLoop, calls=%fused_computation.3 | loop fusion | flops 1048576 | bytes 1065472 | tf_op jit(solution)/shard_map/convert_element_type | solution.py:220
  8.6 1.4 %copy.22.rate_ref = f32[64,1]{1,0:T(8,128)} copy(f32[64,1]{0,1:T(1,128)} %bitcast.33) | data formatting | bytes 512 | tf_op jit(solution)/shard_map/broadcast_in_dim | solution.py:217
  9.9 1.3 %broadcast_in_dim.8.bx_ref.bb_ref.bc_ref = bf16[1,5120]{1,0:T(2,128)(2,1)} reshape(bf16[5120]{0:T(1024)(128)(2,1)} %param.11) | data formatting | bytes 20480 | tf_op jit(solution)/shard_map/broadcast_in_dim | solution.py:221
  11.2 2.9 %shard_map.94 = (f32[4,512,16]{2,1,0:T(8,128)}, f32[64,512]{1,0:T(8,128)}, bf16[512,128]{1,0:T(8,128)(2,1)}, bf16[512,128]{1,0:T(8,128)(2,1)}, bf16[512,128]{1,0:T(8,128)(2,1)}, /*index=5*/bf16[16,128]{1,0:T(8,128)(2,1)}) custom-call(f32[64,512]{1,0:T(8,128)} %bitcast.29, f32[64,1]{1,0:T(8,128)} %copy.22.rate_ref), custom_call_target="tpu_custom_call" | custom-call | flops 10000000 | bytes 1000000 | tf_op jit(solution)/shard_map/pallas_call | solution.py:206
  14.2 0.8 copy.24
  15.0 0.1 copy.25
  15.1 0.6 copy.23
  15.7 2.5 %reshape.94 = bf16[8,20,128]{2,1,0:T(8,128)(2,1)S(1)} reshape(bf16[5120,4]{1,0:T(8,128)(2,1)S(1)} %copy.23) | data formatting | bytes 81920 | tf_op jit(solution)/shard_map/reshape | solution.py:271
  18.2 0.0 collective-permute-done.hx_ref.hb_ref.hc_ref
  18.2 0.0 copy-start.3
  18.2 0.6 copy-done.3
  18.8 18.8 %shard_map.95 = (bf16[512,4096]{1,0:T(8,128)(2,1)}, bf16[512,512]{1,0:T(8,128)(2,1)}, bf16[512,512]{1,0:T(8,128)(2,1)}, bf16[4,128,4096]{2,1,0:T(8,128)(2,1)}, b...) custom-call(bf16[512,5120]{1,0:T(8,128)(2,1)} %bitcast.19, bf16[512,5120]{1,0:T(8,128)(2,1)} %bitcast.20, ...), custom_call_target="tpu_custom_call" | custom-call | flops 1000000000 | bytes 20000000 | tf_op jit(solution)/shard_map/pallas_call | solution.py:237
  37.6 2.4 %fusion.1 = bf16[8,548,128]{2,1,0:T(8,128)(2,1)} fusion(bf16[8,16,8]{2,1,0:T(8,128)(2,1)S(1)} %bitcast.28, bf16[8,20,128]{2,1,0:T(8,128)(2,1)S(1)} %reshape.94, bf16[8,512,128]{2,1,0:T(8,128)(2,1)} %bitcast.26), kind=kLoop, calls=%fused_computation.4 | loop fusion | flops 4489216 | bytes 2213888 | tf_op jit(solution)/shard_map/concatenate | solution.py:274
  40.0 4.9 %all-to-all-start = ((bf16[8,548,128]{2,1,0:T(8,128)(2,1)}), bf16[8,548,128]{2,1,0:T(8,128)(2,1)S(1)}, u32[]{:S(2)}, u32[]{:S(2)}) async-start(bf16[8,548,128]{2,1,0:T(8,128)(2,1)} %fusion.1), calls=%async_computation | async-start | bytes 2260992 | tf_op jit(solution)/shard_map/all_to_all | solution.py:275
  44.8 3.5 %collective-permute-start.1 = (bf16[144,4096]{1,0:T(8,128)(2,1)}, bf16[144,4096]{1,0:T(8,128)(2,1)S(1)}, u32[]{:S(2)}, u32[]{:S(2)}) collective-permute-start(bf16[144,4096]{1,0:T(8,128)(2,1)} %get-tuple-element.32), channel_id=1, source_target_pairs={{0,8},{8,16},{16,24},{1,9},{9,17},{17,25},{2,10},{10,18},{18,26},{... | collective-permute-start | bytes 3538952 | tf_op jit(solution)/shard_map/ppermute | solution.py:203
  48.3 1.9 %collective-permute-start.2 = (bf16[144,4096]{1,0:T(8,128)(2,1)}, bf16[144,4096]{1,0:T(8,128)(2,1)S(1)}, u32[]{:S(2)}, u32[]{:S(2)}) collective-permute-start(bf16[144,4096]{1,0:T(8,128)(2,1)} %get-tuple-element.32), channel_id=1, source_target_pairs={{0,16},{8,24},{1,17},{9,25},{2,18},{10,26},{3,19},{11,27},{4,20},{... | collective-permute-start | bytes 3538952 | tf_op jit(solution)/shard_map/ppermute | solution.py:203
  50.3 2.3 %collective-permute-start.3 = (bf16[144,4096]{1,0:T(8,128)(2,1)}, bf16[144,4096]{1,0:T(8,128)(2,1)}, u32[]{:S(2)}, u32[]{:S(2)}) collective-permute-start(bf16[144,4096]{1,0:T(8,128)(2,1)} %get-tuple-element.32), channel_id=1, source_target_pairs={{0,24},{1,25},{2,26},{3,27},{4,28},{5,29},{6,30},{7,31}} | collective-permute-start | bytes 3538952 | tf_op jit(solution)/shard_map/ppermute | solution.py:203
  52.6 17.0 %shard_map.96.y_ref = f32[512,4096]{1,0:T(8,128)} custom-call(bf16[512,4096]{1,0:T(8,128)(2,1)} %get-tuple-element.23.x_ref, bf16[512,512]{1,0:T(8,128)(2,1)} %get-tuple-element.24.b_ref, bf16[512,512]{1,0:T(8,128)(2,1)} %get-tuple-element.25.c_ref, bf16[4,128,4096]{2,1,0:T(8,128)(2,1)} %get-tuple-element.26.prev_ref, ...), custom_call_target="tpu_custom_call" | custom-call | flops 4000000000 | bytes 40000000 | tf_op jit(solution)/shard_map/pallas_call | solution.py:277
  69.6 3.6 %all-to-all-done.got_ref = bf16[8,548,128]{2,1,0:T(8,128)(2,1)S(1)} async-done(((bf16[8,548,128]{2,1,0:T(8,128)(2,1)}), bf16[8,548,128]{2,1,0:T(8,128)(2,1)S(1)}, u32[]{:S(2)}, u32[]{:S(2)}) %all-to-all-start) | async-done | bytes 1122336 | tf_op jit(solution)/shard_map/all_to_all | solution.py:275
  73.2 0.0 copy-start
  73.2 1.0 copy-done
  74.2 5.9 %shard_map.97 = bf16[8,548,128]{2,1,0:T(8,128)(2,1)} custom-call(s32[8]{0:T(128)} %slot_ref.1, bf16[8,548,128]{2,1,0:T(8,128)(2,1)} %copy-done), custom_call_target="tpu_custom_call" | custom-call | flops 1000000 | bytes 2000000 | tf_op jit(solution)/shard_map/pallas_call | solution.py:293
  80.0 3.5 %all-to-all-start.1 = ((bf16[8,548,128]{2,1,0:T(8,128)(2,1)}), bf16[8,548,128]{2,1,0:T(8,128)(2,1)S(1)}, u32[]{:S(2)}, u32[]{:S(2)}) async-start(bf16[8,548,128]{2,1,0:T(8,128)(2,1)} %shard_map.97), calls=%async_computation.1 | async-start | bytes 2260992 | tf_op jit(solution)/shard_map/all_to_all | solution.py:304
  83.6 0.0 collective-permute-done.1.rest_0_
  83.6 0.0 copy-start.1
  83.6 23.1 %collective-permute-done.2.rest_1_ = bf16[144,4096]{1,0:T(8,128)(2,1)S(1)} collective-permute-done((bf16[144,4096]{1,0:T(8,128)(2,1)}, bf16[144,4096]{1,0:T(8,128)(2,1)S(1)}, u32[]{:S(2)}, u32[]{:S(2)}) %collective-permute-start.2) | collective-permute-done | bytes 1179680 | tf_op jit(solution)/shard_map/ppermute | solution.py:203
  106.7 0.0 copy-start.2
  106.7 0.0 collective-permute-done.3.rest_2_
  106.7 0.0 copy-done.1
  106.7 1.0 copy-done.2
  107.8 9.5 %shard_map.98 = bf16[512,4096]{1,0:T(8,128)(2,1)} custom-call(f32[512,4096]{1,0:T(8,128)} %shard_map.96.y_ref, bf16[512,512]{1,0:T(8,128)(2,1)} %get-tuple-element.25.c_ref, bf16[512,128]{1,0:T(8,128)(2,1)} %get-tuple-element.31.full_ref, bf16[128,4096]{1,0:T(8,128)(2,1)} %compare_convert_fusion.exp_ref, f32[1,4096]{1,0:T(1,128)} %bitcast.31, ...), custom_call_target="tpu_custom_call" | custom-call | flops 1000000000 | bytes 20000000 | tf_op jit(solution)/shard_map/pallas_call | solution.py:307
  117.3 0.0 all-to-all-done.1
  117.3 0.1 multiply_reduce_fusion.1
  117.5 0.1 mul.29
  117.5 0.1 mul.30
  117.6 1.5 %multiply_reduce_fusion = f32[2,512,128]{2,1,0:T(8,128)} fusion(bf16[4,2,548,128]{3,2,1,0:T(8,128)(2,1)S(1)} %bitcast.24, f32[4,2,512]{2,1,0:T(2,128)S(1)} %mul.30), kind=kLoop, calls=%fused_computation.2 | loop fusion | flops 1441792 | bytes 1589248 | tf_op jit(solution)/shard_map/reduce_sum | solution.py:330
  119.1 0.7 reshape_squeeze.3
  119.9 0.8 copy.27
  (7 shorter events, 0.1 us)
Async XLA Ops:
  1.5 16.7 %collective-permute-start = (bf16[8,5120]{1,0:T(8,128)(2,1)S(1)}, bf16[8,5120]{1,0:T(8,128)(2,1)S(1)}, u32[]{:S(2)}, u32[]{:S(2)}) collective-permute-start(bf16[8,5120]{1,0:T(8,128)(2,1)S(1)} %slice_bitcast_fusion), channel_id=1, source_target_pairs={{0,8},{8,16},{16,24},{1,9},{9,17},{17,25},{2,10},{10,18},{18,26},{... | collective-permute-start | bytes 245768 | tf_op jit(solution)/shard_map/ppermute | solution.py:203
  18.2 0.6 copy-start.3
  40.0 33.2 %all-to-all-start = ((bf16[8,548,128]{2,1,0:T(8,128)(2,1)}), bf16[8,548,128]{2,1,0:T(8,128)(2,1)S(1)}, u32[]{:S(2)}, u32[]{:S(2)}) async-start(bf16[8,548,128]{2,1,0:T(8,128)(2,1)} %fusion.1), calls=%async_computation | async-start | bytes 2260992 | tf_op jit(solution)/shard_map/all_to_all | solution.py:275
  44.8 38.8 %collective-permute-start.1 = (bf16[144,4096]{1,0:T(8,128)(2,1)}, bf16[144,4096]{1,0:T(8,128)(2,1)S(1)}, u32[]{:S(2)}, u32[]{:S(2)}) collective-permute-start(bf16[144,4096]{1,0:T(8,128)(2,1)} %get-tuple-element.32), channel_id=1, source_target_pairs={{0,8},{8,16},{16,24},{1,9},{9,17},{17,25},{2,10},{10,18},{18,26},{... | collective-permute-start | bytes 3538952 | tf_op jit(solution)/shard_map/ppermute | solution.py:203
  48.3 58.4 %collective-permute-start.2 = (bf16[144,4096]{1,0:T(8,128)(2,1)}, bf16[144,4096]{1,0:T(8,128)(2,1)S(1)}, u32[]{:S(2)}, u32[]{:S(2)}) collective-permute-start(bf16[144,4096]{1,0:T(8,128)(2,1)} %get-tuple-element.32), channel_id=1, source_target_pairs={{0,16},{8,24},{1,17},{9,25},{2,18},{10,26},{3,19},{11,27},{4,20},{... | collective-permute-start | bytes 3538952 | tf_op jit(solution)/shard_map/ppermute | solution.py:203
  50.3 56.5 %collective-permute-start.3 = (bf16[144,4096]{1,0:T(8,128)(2,1)}, bf16[144,4096]{1,0:T(8,128)(2,1)}, u32[]{:S(2)}, u32[]{:S(2)}) collective-permute-start(bf16[144,4096]{1,0:T(8,128)(2,1)} %get-tuple-element.32), channel_id=1, source_target_pairs={{0,24},{1,25},{2,26},{3,27},{4,28},{5,29},{6,30},{7,31}} | collective-permute-start | bytes 3538952 | tf_op jit(solution)/shard_map/ppermute | solution.py:203
  73.2 1.0 copy-start
  80.0 37.2 %all-to-all-start.1 = ((bf16[8,548,128]{2,1,0:T(8,128)(2,1)}), bf16[8,548,128]{2,1,0:T(8,128)(2,1)S(1)}, u32[]{:S(2)}, u32[]{:S(2)}) async-start(bf16[8,548,128]{2,1,0:T(8,128)(2,1)} %shard_map.97), calls=%async_computation.1 | async-start | bytes 2260992 | tf_op jit(solution)/shard_map/all_to_all | solution.py:304
  83.6 23.1 %copy-start.1 = (bf16[144,4096]{1,0:T(8,128)(2,1)}, bf16[144,4096]{1,0:T(8,128)(2,1)S(1)}, u32[]{:S(2)}) copy-start(bf16[144,4096]{1,0:T(8,128)(2,1)S(1)} %collective-permute-done.1.rest_0_) | copy-start | bytes 3538948
  106.7 1.0 copy-start.2

commit v3 on v2

--- a/solution.py
+++ b/solution.py
@@ -3,10 +3,12 @@
 
 import jax
 import jax.numpy as jnp
+import numpy as np
 from jax import lax
 from jax.experimental import pallas as pl
 from jax.experimental.pallas import tpu as pltpu
 from jax.sharding import PartitionSpec as P
+
 
 HEAD_DIM = 64
 STATE = 128
@@ -34,11 +36,12 @@
     upper = jnp.where(u <= t, 1.0, 0.0).astype(F32)
     base = jnp.zeros((heads, 1), F32)
     log = jnp.zeros((1, heads), F32)
+    slope = jnp.broadcast_to(rate_ref[...] * -LOG2E, (heads, heads)).T[:, 0:1]
     for j in range(length // SUB):
         cut = slice(j * SUB, (j + 1) * SUB)
         raw = raw_ref[:, cut]
         dt = jnp.maximum(raw, 0.0) + jnp.log(1.0 + jnp.exp(-jnp.abs(raw)))
-        rate = dt * (rate_ref[...] * -LOG2E)
+        rate = dt * slope
         cs = jnp.dot(rate, upper, precision=lax.Precision.HIGHEST, preferred_element_type=F32)
         q = cs - jnp.log(dt) * LOG2E
         row_ref[:, cut] = q
@@ -185,9 +188,8 @@
     return pl.CostEstimate(flops=flops, bytes_accessed=nbytes, transcendentals=0)
 
 
-def body(conv_input, step_raw, decay_rate, conv_weight, conv_bias, norm_gain, owner_slot):
+def layer(conv_input, step_raw, decay_rate, conv_weight, conv_bias, norm_gain, owner_slot):
     seq, ngrp = lax.axis_size("seq"), lax.axis_size("grp")
-    place = lax.axis_index("seq")
     width = conv_weight.shape[0]
     rows = conv_input[0]
     length, chans = rows.shape
@@ -202,7 +204,8 @@
     def along(value, distance):
         return lax.ppermute(value, "seq", [(i, i + distance) for i in range(seq - distance)])
 
-    halo = along(rows[length - HALO :], 1)
+    last_rows = rows[length - HALO :]
+    halo = along(last_rows, 1)
     cols_t, rows_q, tail, near, full, shard_log = pl.pallas_call(
         step_kernel,
         out_shape=(
@@ -214,10 +217,10 @@
             shape((LOG_ROWS, 2 * heads), BF16),
         ),
         cost_estimate=cost(10**7, 10**6),
-    )(step_raw[0], decay_rate[:, None])
-
-    picks = jnp.arange(2 * heads)[:, None] % heads == jnp.arange(d_in)[None, :] // HEAD_DIM
-    expand = picks.astype(BF16)
+    )(step_raw[0], decay_rate[None, :])
+
+    picks = np.arange(2 * heads)[:, None] % heads == np.arange(d_in)[None, :] // HEAD_DIM
+    expand = jnp.asarray(picks.astype(BF16))
     bias = conv_bias[None, :]
     b_at, c_at = d_in // STATE, d_in // STATE + GROUPS
 
@@ -265,14 +268,9 @@
         bias, bias, bias, tail, near, shard_log, expand,
     )
 
-    got = [along(end, k) for k in range(1, seq)]
-
-    sent_state = end_t.reshape(ngrp, -1, STATE)
-    kept = rows[length - width :].T.reshape(ngrp, -1, STATE)
-    log_terms = shard_log[:, :heads].reshape(LOG_ROWS, ngrp, -1).swapaxes(0, 1)
-    log_terms = jnp.pad(log_terms, ((0, 0), (0, 0), (0, STATE - log_terms.shape[2])))
-    sent = jnp.concatenate([sent_state, kept, log_terms], axis=1)
-    swapped = lax.all_to_all(sent, "grp", split_axis=0, concat_axis=0, tiled=True)
+    got = []
+    for k in range(1, seq):
+        got.append(along(end, k))
 
     y = pl.pallas_call(
         intra_kernel,
@@ -288,7 +286,14 @@
         cost_estimate=cost(4 * 10**9, 4 * 10**7),
     )(xc, bc, cc, prev, cols_t, rows_q, near, expand)
 
-    swapped, y = lax.optimization_barrier((swapped, y))
+
+    end_t, last_rows, shard_log, y = lax.optimization_barrier((end_t, last_rows, shard_log, y))
+    sent_state = end_t.reshape(ngrp, -1, STATE)
+    kept = last_rows[HALO - width :].T.reshape(ngrp, -1, STATE)
+    log_terms = shard_log[:, :heads].reshape(LOG_ROWS, ngrp, -1).swapaxes(0, 1)
+    log_terms = jnp.pad(log_terms, ((0, 0), (0, 0), (0, STATE - log_terms.shape[2])))
+    sent = jnp.concatenate([sent_state, kept, log_terms], axis=1)
+    swapped = lax.all_to_all(sent, "grp", split_axis=0, concat_axis=0, tiled=True)
     tallness = sent.shape[1]
     placed = pl.pallas_call(
         place_kernel,
@@ -301,6 +306,7 @@
         out_shape=shape(swapped.shape, BF16),
         cost_estimate=cost(10**6, 2 * 10**6),
     )(owner_slot, swapped)
+    placed, got = lax.optimization_barrier((placed, got))
     owned = lax.all_to_all(placed, "seq", split_axis=0, concat_axis=0, tiled=True)
 
     hops = seq - 1
@@ -335,7 +341,7 @@
 def solution(mesh):
     placed = (P("grp", "seq", None), P("grp", None, "seq"), P(), P(), P(), P(), P())
     return jax.shard_map(
-        body,
+        layer,
         mesh=mesh,
         in_specs=placed,
         out_specs=(P("grp", "seq", None), P("seq", "grp", None, None), P("seq", "grp", None)),

time: 122 us -> 136 us (1.11)
  waiting for transfers between devices: 26.7 us -> 45.8 us
  local copies, waits for them, and re-layouts: 12.8 us -> 8.86 us
  other arithmetic: 5.26 us -> 2.74 us
  starting transfers between devices: 21 us -> 22.6 us
    all_to_all x2, waiting for transfers between devices: 3.57 us -> 25.2 us  [the longest x1 20.4 us: layer(): lax.all_to_all(sent, 'grp', split_axis=0, concat_axis=0, tiled=True)]
    ppermute x4, waiting for transfers between devices: 23.1 us -> 20.6 us  [along(): lax.ppermute(value, 'seq', [(i, i + distance) for i in range(seq - distan...]
    all_to_all x2, starting transfers between devices: 8.4 us -> 9.83 us  [the longest x1 4.95 us: layer(): lax.all_to_all(placed, 'seq', split_axis=0, concat_axis=0, tiled=True)]
    unnamed x9 -> x13, local copies, waits for them, and re-layouts: 3.44 us -> 2.41 us
  transfers between devices with their start and end apart: 6 -> 6, of which waited for: 2 -> 3; matrix products, arithmetic and copies ran while one was open for 7% -> 1% of each run, Pallas kernels for 29% -> 14%
where the time goes in v3:
time: 136 us; the launch traced here: 135 us
  Pallas kernels  54.2 us (40%)
  waiting for transfers between devices  45.8 us (34%)
  starting transfers between devices  22.6 us (17%)
  local copies, waits for them, and re-layouts  8.86 us (7%)
  other arithmetic  2.74 us (2%)
    ppermute x4, waiting for transfers between devices, along(): lax.ppermute(value, 'seq', [(i, i + distance) for i in range(seq - distan...  20.6 us
    all_to_all x1, waiting for transfers between devices, layer(): lax.all_to_all(sent, 'grp', split_axis=0, concat_axis=0, tiled=True)  20.4 us
    pallas_call x1, Pallas kernels, layer(): pl.pallas_call(state_kernel, grid=(GROUPS,), in_specs=trio(length) + trio...  18.7 us
    pallas_call x1, Pallas kernels, layer(): pl.pallas_call(intra_kernel, grid=(GROUPS, blocks), in_specs=[x_spec(SUB,...  17 us
    ppermute x4, starting transfers between devices, along(): lax.ppermute(value, 'seq', [(i, i + distance) for i in range(seq - distan...  12.7 us
    pallas_call x1, Pallas kernels, layer(): pl.pallas_call(functools.partial(norm_kernel, hops), grid=(GROUPS,), in_s...  9.55 us
    pallas_call x1, Pallas kernels, layer(): pl.pallas_call(place_kernel, grid_spec=pltpu.PrefetchScalarGridSpec(num_s...  5.91 us
    all_to_all x1, starting transfers between devices, layer(): lax.all_to_all(placed, 'seq', split_axis=0, concat_axis=0, tiled=True)  4.95 us
  transfers between devices with their start and end apart: 6, of which 3 were waited for; matrix products, arithmetic and copies ran while one was open for 1% of the time, Pallas kernels for 14%

profile of v3, /device:TPU:0, one launch (start us, length us, event | category | flops | bytes accessed | tf_op | source)
XLA Modules:
  0.0 134.9 jit_solution(14300792743611796140)
XLA Ops:
  0.6 0.9 slice_bitcast_fusion
  1.5 4.9 %collective-permute-start = (bf16[8,5120]{1,0:T(8,128)(2,1)S(1)}, bf16[8,5120]{1,0:T(8,128)(2,1)S(1)}, u32[]{:S(2)}, u32[]{:S(2)}) collective-permute-start(bf16[8,5120]{1,0:T(8,128)(2,1)S(1)} %slice_bitcast_fusion), channel_id=1, source_target_pairs={{0,8},{8,16},{16,24},{1,9},{9,17},{17,25},{2,10},{10,18},{18,26},{... | collective-permute-start | bytes 245768 | tf_op jit(solution)/shard_map/ppermute | solution.py:205
  6.4 1.3 broadcast_in_dim.8.bx_ref.bb_ref.bc_ref
  7.7 3.0 %shard_map.103 = (f32[4,512,16]{2,1,0:T(8,128)}, f32[64,512]{1,0:T(8,128)}, bf16[512,128]{1,0:T(8,128)(2,1)}, bf16[512,128]{1,0:T(8,128)(2,1)}, bf16[512,128]{1,0:T(8,128)(2,1)}, /*index=5*/bf16[16,128]{1,0:T(8,128)(2,1)}) custom-call(f32[64,512]{1,0:T(8,128)} %bitcast.27, f32[1,64]{1,0:T(1,128)} %bitcast.31), custom_call_target="tpu_custom_call" | custom-call | flops 10000000 | bytes 1000000 | tf_op jit(solution)/shard_map/pallas_call | solution.py:209
  10.7 0.0 collective-permute-done.hx_ref.hb_ref.hc_ref
  10.7 0.0 copy-start.4
  10.7 0.6 copy-done.4
  11.4 18.7 %shard_map.104 = (bf16[512,4096]{1,0:T(8,128)(2,1)}, bf16[512,512]{1,0:T(8,128)(2,1)}, bf16[512,512]{1,0:T(8,128)(2,1)}, bf16[4,128,4096]{2,1,0:T(8,128)(2,1)}, ...) custom-call(bf16[512,5120]{1,0:T(8,128)(2,1)} %bitcast.17, bf16[512,5120]{1,0:T(8,128)(2,1)} %bitcast.18, ...), custom_call_target="tpu_custom_call" | custom-call | flops 1000000000 | bytes 20000000 | tf_op jit(solution)/shard_map/pallas_call | solution.py:240
  30.1 17.0 %shard_map.105.y_ref = f32[512,4096]{1,0:T(8,128)} custom-call(bf16[512,4096]{1,0:T(8,128)(2,1)} %get-tuple-element.29.x_ref, bf16[512,512]{1,0:T(8,128)(2,1)} %get-tuple-element.30.b_ref, bf16[512,512]{1,0:T(8,128)(2,1)} %get-tuple-element.31.c_ref, bf16[4,128,4096]{2,1,0:T(8,128)(2,1)} %get-tuple-element.32.prev_ref, ...), custom_call_target="tpu_custom_call" | custom-call | flops 4000000000 | bytes 40000000 | tf_op jit(solution)/shard_map/pallas_call | solution.py:275
  47.2 0.0 copy-start.5
  47.2 0.0 copy-start.3
  47.2 0.6 copy.20
  47.8 2.5 %reshape.41 = bf16[8,20,128]{2,1,0:T(8,128)(2,1)S(1)} reshape(bf16[5120,4]{1,0:T(8,128)(2,1)S(1)} %copy.20) | data formatting | bytes 81920 | tf_op jit(solution)/shard_map/reshape | solution.py:292
  50.3 0.0 copy-done.5
  50.3 0.1 copy.21
  50.4 0.1 copy.22
  50.5 0.0 copy-done.3
  50.5 1.1 fusion.1
  51.6 4.9 %all-to-all-start = ((bf16[8,548,128]{2,1,0:T(8,128)(2,1)}), bf16[8,548,128]{2,1,0:T(8,128)(2,1)S(1)}, u32[]{:S(2)}, u32[]{:S(2)}) async-start(bf16[8,548,128]{2,1,0:T(8,128)(2,1)} %fusion.1), calls=%async_computation | async-start | bytes 2260992 | tf_op jit(solution)/shard_map/all_to_all | solution.py:296
  56.5 3.5 %collective-permute-start.1 = (bf16[144,4096]{1,0:T(8,128)(2,1)}, bf16[144,4096]{1,0:T(8,128)(2,1)S(1)}, u32[]{:S(2)}, u32[]{:S(2)}) collective-permute-start(bf16[144,4096]{1,0:T(8,128)(2,1)} %get-tuple-element.38), channel_id=1, source_target_pairs={{0,8},{8,16},{16,24},{1,9},{9,17},{17,25},{2,10},{10,18},{18,26},{... | collective-permute-start | bytes 3538952 | tf_op jit(solution)/shard_map/ppermute | solution.py:205
  60.0 2.0 %collective-permute-start.2 = (bf16[144,4096]{1,0:T(8,128)(2,1)}, bf16[144,4096]{1,0:T(8,128)(2,1)S(1)}, u32[]{:S(2)}, u32[]{:S(2)}) collective-permute-start(bf16[144,4096]{1,0:T(8,128)(2,1)} %get-tuple-element.38), channel_id=1, source_target_pairs={{0,16},{8,24},{1,17},{9,25},{2,18},{10,26},{3,19},{11,27},{4,20},{... | collective-permute-start | bytes 3538952 | tf_op jit(solution)/shard_map/ppermute | solution.py:205
  62.0 2.4 %collective-permute-start.3 = (bf16[144,4096]{1,0:T(8,128)(2,1)}, bf16[144,4096]{1,0:T(8,128)(2,1)}, u32[]{:S(2)}, u32[]{:S(2)}) collective-permute-start(bf16[144,4096]{1,0:T(8,128)(2,1)} %get-tuple-element.38), channel_id=1, source_target_pairs={{0,24},{1,25},{2,26},{3,27},{4,28},{5,29},{6,30},{7,31}} | collective-permute-start | bytes 3538952 | tf_op jit(solution)/shard_map/ppermute | solution.py:205
  64.4 20.4 %all-to-all-done.got_ref = bf16[8,548,128]{2,1,0:T(8,128)(2,1)S(1)} async-done(((bf16[8,548,128]{2,1,0:T(8,128)(2,1)}), bf16[8,548,128]{2,1,0:T(8,128)(2,1)S(1)}, u32[]{:S(2)}, u32[]{:S(2)}) %all-to-all-start) | async-done | bytes 1122336 | tf_op jit(solution)/shard_map/all_to_all | solution.py:296
  84.8 0.0 copy-start
  84.8 1.0 copy-done
  85.8 5.9 %shard_map.106 = bf16[8,548,128]{2,1,0:T(8,128)(2,1)} custom-call(s32[8]{0:T(128)} %slot_ref.1, bf16[8,548,128]{2,1,0:T(8,128)(2,1)} %copy-done), custom_call_target="tpu_custom_call" | custom-call | flops 1000000 | bytes 2000000 | tf_op jit(solution)/shard_map/pallas_call | solution.py:298
  91.7 0.0 collective-permute-done.1.rest_0_
  91.7 0.0 copy-start.1
  91.7 20.6 %collective-permute-done.2.rest_1_ = bf16[144,4096]{1,0:T(8,128)(2,1)S(1)} collective-permute-done((bf16[144,4096]{1,0:T(8,128)(2,1)}, bf16[144,4096]{1,0:T(8,128)(2,1)S(1)}, u32[]{:S(2)}, u32[]{:S(2)}) %collective-permute-start.2) | collective-permute-done | bytes 1179680 | tf_op jit(solution)/shard_map/ppermute | solution.py:205
  112.3 0.0 copy-start.2
  112.3 0.0 collective-permute-done.3.rest_2_
  112.3 4.9 %all-to-all-start.1 = ((bf16[8,548,128]{2,1,0:T(8,128)(2,1)}), bf16[8,548,128]{2,1,0:T(8,128)(2,1)S(1)}, u32[]{:S(2)}, u32[]{:S(2)}) async-start(bf16[8,548,128]{2,1,0:T(8,128)(2,1)} %shard_map.106), calls=%async_computation.1 | async-start | bytes 2260992 | tf_op jit(solution)/shard_map/all_to_all | solution.py:310
  117.2 0.0 copy-done.1
  117.3 0.0 copy-done.2
  117.3 9.6 %shard_map.107 = bf16[512,4096]{1,0:T(8,128)(2,1)} custom-call(f32[512,4096]{1,0:T(8,128)} %shard_map.105.y_ref, bf16[512,512]{1,0:T(8,128)(2,1)} %get-tuple-element.31.c_ref, bf16[512,128]{1,0:T(8,128)(2,1)} %get-tuple-element.41.full_ref, bf16[128,4096]{1,0:T(8,128)(2,1)} %constant.9.clone.exp_ref, f32[1,4096]{1,0:T(1,128)} %bitcast.29, ...), custom_call_target="tpu_custom_call" | custom-call | flops 1000000000 | bytes 20000000 | tf_op jit(solution)/shard_map/pallas_call | solution.py:313
  126.8 4.8 %all-to-all-done.1 = bf16[8,548,128]{2,1,0:T(8,128)(2,1)S(1)} async-done(((bf16[8,548,128]{2,1,0:T(8,128)(2,1)}), bf16[8,548,128]{2,1,0:T(8,128)(2,1)S(1)}, u32[]{:S(2)}, u32[]{:S(2)}) %all-to-all-start.1) | async-done | bytes 1122336 | tf_op jit(solution)/shard_map/all_to_all | solution.py:310
  131.6 0.1 multiply_reduce_fusion.1
  131.7 0.1 mul.29
  131.8 0.1 mul.30
  131.9 1.5 %multiply_reduce_fusion = f32[2,512,128]{2,1,0:T(8,128)} fusion(bf16[4,2,548,128]{3,2,1,0:T(8,128)(2,1)S(1)} %bitcast.22, f32[4,2,512]{2,1,0:T(2,128)S(1)} %mul.30), kind=kLoop, calls=%fused_computation.2 | loop fusion | flops 1441792 | bytes 1589248 | tf_op jit(solution)/shard_map/reduce_sum | solution.py:336
  133.4 0.7 reshape_squeeze.3
  134.1 0.8 copy.24
  (6 shorter events, 0.1 us)
Async XLA Ops:
  1.5 9.2 %collective-permute-start = (bf16[8,5120]{1,0:T(8,128)(2,1)S(1)}, bf16[8,5120]{1,0:T(8,128)(2,1)S(1)}, u32[]{:S(2)}, u32[]{:S(2)}) collective-permute-start(bf16[8,5120]{1,0:T(8,128)(2,1)S(1)} %slice_bitcast_fusion), channel_id=1, source_target_pairs={{0,8},{8,16},{16,24},{1,9},{9,17},{17,25},{2,10},{10,18},{18,26},{... | collective-permute-start | bytes 245768 | tf_op jit(solution)/shard_map/ppermute | solution.py:205
  10.7 0.6 copy-start.4
  47.2 3.2 %copy-start.5 = (bf16[16,128]{1,0:T(8,128)(2,1)S(1)}, bf16[16,128]{1,0:T(8,128)(2,1)}, u32[]{:S(2)}) copy-start(bf16[16,128]{1,0:T(8,128)(2,1)} %get-tuple-element.37.log_ref) | copy-start | bytes 12292
  47.2 3.3 %copy-start.3 = (bf16[4096,128]{1,0:T(8,128)(2,1)S(1)}, bf16[4096,128]{1,0:T(8,128)(2,1)}, u32[]{:S(2)}) copy-start(bf16[4096,128]{1,0:T(8,128)(2,1)} %get-tuple-element.35) | copy-start | bytes 3145732
  51.6 33.2 %all-to-all-start = ((bf16[8,548,128]{2,1,0:T(8,128)(2,1)}), bf16[8,548,128]{2,1,0:T(8,128)(2,1)S(1)}, u32[]{:S(2)}, u32[]{:S(2)}) async-start(bf16[8,548,128]{2,1,0:T(8,128)(2,1)} %fusion.1), calls=%async_computation | async-start | bytes 2260992 | tf_op jit(solution)/shard_map/all_to_all | solution.py:296
  56.5 35.2 %collective-permute-start.1 = (bf16[144,4096]{1,0:T(8,128)(2,1)}, bf16[144,4096]{1,0:T(8,128)(2,1)S(1)}, u32[]{:S(2)}, u32[]{:S(2)}) collective-permute-start(bf16[144,4096]{1,0:T(8,128)(2,1)} %get-tuple-element.38), channel_id=1, source_target_pairs={{0,8},{8,16},{16,24},{1,9},{9,17},{17,25},{2,10},{10,18},{18,26},{... | collective-permute-start | bytes 3538952 | tf_op jit(solution)/shard_map/ppermute | solution.py:205
  60.0 52.3 %collective-permute-start.2 = (bf16[144,4096]{1,0:T(8,128)(2,1)}, bf16[144,4096]{1,0:T(8,128)(2,1)S(1)}, u32[]{:S(2)}, u32[]{:S(2)}) collective-permute-start(bf16[144,4096]{1,0:T(8,128)(2,1)} %get-tuple-element.38), channel_id=1, source_target_pairs={{0,16},{8,24},{1,17},{9,25},{2,18},{10,26},{3,19},{11,27},{4,20},{... | collective-permute-start | bytes 3538952 | tf_op jit(solution)/shard_map/ppermute | solution.py:205
  62.0 50.3 %collective-permute-start.3 = (bf16[144,4096]{1,0:T(8,128)(2,1)}, bf16[144,4096]{1,0:T(8,128)(2,1)}, u32[]{:S(2)}, u32[]{:S(2)}) collective-permute-start(bf16[144,4096]{1,0:T(8,128)(2,1)} %get-tuple-element.38), channel_id=1, source_target_pairs={{0,24},{1,25},{2,26},{3,27},{4,28},{5,29},{6,30},{7,31}} | collective-permute-start | bytes 3538952 | tf_op jit(solution)/shard_map/ppermute | solution.py:205
  84.8 1.0 copy-start
  91.7 25.5 %copy-start.1 = (bf16[144,4096]{1,0:T(8,128)(2,1)}, bf16[144,4096]{1,0:T(8,128)(2,1)S(1)}, u32[]{:S(2)}) copy-start(bf16[144,4096]{1,0:T(8,128)(2,1)S(1)} %collective-permute-done.1.rest_0_) | copy-start | bytes 3538948
  112.3 5.0 %copy-start.2 = (bf16[144,4096]{1,0:T(8,128)(2,1)}, bf16[144,4096]{1,0:T(8,128)(2,1)S(1)}, u32[]{:S(2)}) copy-start(bf16[144,4096]{1,0:T(8,128)(2,1)S(1)} %collective-permute-done.2.rest_1_) | copy-start | bytes 3538948
  112.3 19.3 %all-to-all-start.1 = ((bf16[8,548,128]{2,1,0:T(8,128)(2,1)}), bf16[8,548,128]{2,1,0:T(8,128)(2,1)S(1)}, u32[]{:S(2)}, u32[]{:S(2)}) async-start(bf16[8,548,128]{2,1,0:T(8,128)(2,1)} %shard_map.106), calls=%async_computation.1 | async-start | bytes 2260992 | tf_op jit(solution)/shard_map/all_to_all | solution.py:310
